TPU v7x, 128 devices: a whole 4x4x4 slice. The times are simulated.
128 devices in a mesh: band: 16 (over x, y_hi, core), grid: 8 (over y_lo, z).
Axes of the slice: x: 4, y: 4 (y_hi: 2, y_lo: 2; y = y_hi * 2 + y_lo), z: 4, core: 2. Of those that a mesh axis runs over, the one named last changes fastest.
Arguments:
- wave: bfloat16 [4096, 20480], P('band', 'grid'), may hold values from -6 to 6
- ritz: bfloat16 [4096, 4096], P('band', 'grid'), may hold values from -0.125 to 0.125
- occupation: float32 [4096], P('band'), may hold values from 0 to 2
Outputs:
- rotated: bfloat16 [4096, 20480], P('band', 'grid')
- density: float32 [20480], P('grid')
All inputs are finite; a program needn't handle non-finite values.
Results may differ from a plain program's by a relative error of at most 0.0017.
Values may be sent and summed in bfloat16 or wider, within the bound.
A program may use at most 128 MiB of HBM per device.

v0:
```python
import jax
import jax.numpy as jnp
from jax import lax
from jax.sharding import PartitionSpec as P

NB = 4096


def copy_for_each(value, axis):
    length = lax.axis_size(axis)
    return lax.all_to_all(
        jnp.broadcast_to(value[None], (length, *value.shape)), axis, 0, 0, tiled=True
    )


def laid_out(tiles, dim):
    shape = list(tiles.shape[1:])
    shape[dim] *= tiles.shape[0]
    return jnp.moveaxis(tiles, 0, dim).reshape(shape)


def collect(value, axis, dim):
    tiles = copy_for_each(value, axis)
    return laid_out(tiles, dim)


def over_copies(value, axis):
    return copy_for_each(value, axis).sum(axis=0)


def per_device(wave, ritz, occupation):
    ritz_rows = collect(ritz, "grid", 1)
    ritz_cols = lax.all_to_all(ritz_rows, "band", split_axis=1, concat_axis=0, tiled=True)
    summed = lax.dot_general(
        ritz_cols,
        lax.all_gather(wave, "band", axis=0, tiled=True),
        (((0,), (0,)), ((), ())),
        preferred_element_type=jnp.float32,
    )
    rotated = summed.astype(jnp.bfloat16)
    values = rotated.astype(jnp.float32)
    partial_terms = jnp.sum(occupation[:, None] * values * values, axis=0)
    density = over_copies(partial_terms, "band") / NB
    return (rotated, density)


def solution(mesh):
    return jax.shard_map(
        per_device,
        mesh=mesh,
        in_specs=(P("band", "grid"), P("band", "grid"), P("band")),
        out_specs=(P("band", "grid"), P("grid")),
        check_vma=False,
    )
```

profile of v0, /device:TPU:1, one launch (start us, length us, event | category | flops | bytes accessed | tf_op | source)
XLA Modules:
  0.0 200.1 jit_solution(17522435744120886784)
XLA Ops:
  7.2 0.0 all-gather.2.cloned.1.call-start
  7.2 0.7 all-gather.2.cloned.1.call-update
  7.9 1.1 copy.9
  9.0 0.1 broadcast_in_dim.4
  9.1 43.4 %all_to_all.30 = bf16[8,256,512]{1,2,0:T(8,128)(2,1)S(1)} all-to-all(bf16[8,256,512]{1,2,0:T(8,128)(2,1)S(1)} %broadcast_in_dim.4), channel_id=1, replica_groups=mesh['band'=16,'grid'=8] {'grid'}, dimensions={0} | all-to-all | bytes 4194304 | tf_op jit(solution)/shard_map/all_to_all | solution.py:11
  52.6 48.4 %all_to_all.31 = bf16[256,16,256]{0,2,1:T(8,128)(2,1)} all-to-all(bf16[256,16,256]{0,2,1:T(8,128)(2,1)S(1)} %bitcast.8), channel_id=1, replica_groups=mesh['band'=16,'grid'=8] {'band'}, dimensions={1} | all-to-all | bytes 4194304 | tf_op jit(solution)/shard_map/all_to_all | solution.py:33
  100.9 0.0 copy-start
  100.9 2.9 %copy.10 = bf16[16,256,256]{2,1,0:T(8,128)(2,1)S(1)} copy(bf16[16,256,256]{1,2,0:T(8,128)(2,1)} %bitcast.9) | data formatting | bytes 4194304 | tf_op jit(solution)/shard_map/all_to_all | solution.py:33
  103.8 66.7 %all-gather.2.cloned.1.call-done = bf16[4096,2560]{1,0:T(8,128)(2,1)} async-done(((bf16[256,2560]{1,0:T(8,128)(2,1)}), bf16[4096,2560]{1,0:T(8,128)(2,1)}) %all-gather.2.cloned.1.call-update) | async-done | bytes 20971536 | tf_op jit(solution)/shard_map/all_gather | solution.py:36
  170.5 0.0 copy-done
  170.5 11.3 %fusion = (f32[2560]{0:T(1024)S(1)}, bf16[256,2560]{1,0:T(8,128)(2,1)}) fusion(f32[256]{0:T(256)S(1)} %copy-done, bf16[4096,256]{1,0:T(8,128)(2,1)S(1)} %bitcast.7, bf16[4096,2560]{1,0:T(8,128)(2,1)} %all-gather.2.cloned.1.call-done), kind=kOutput, calls=%fused_computation.2 | convolution fusion | flops 5371983360 | bytes 24390656 | tf_op jit(solution)/shard_map/dot_general | solution.py:34
  181.8 0.1 broadcast_in_dim.5
  181.9 10.7 %all_to_all.32 = f32[16,1,2560]{2,1,0:T(1,128)S(1)} all-to-all(f32[16,1,2560]{2,1,0:T(1,128)S(1)} %broadcast_in_dim.5), channel_id=1, replica_groups=mesh['band'=16,'grid'=8] {'band'}, dimensions={0} | all-to-all | bytes 327680 | tf_op jit(solution)/shard_map/all_to_all | solution.py:11
  192.6 0.1 reduce_sum.19
  192.7 0.6 broadcast_multiply_fusion
Async XLA Ops:
  7.2 163.3 %all-gather.2.cloned.1.call-start = ((), (), s32[]{:S(2)}) async-start(), calls=%async_computation.3 | async-start | bytes 22282240 | tf_op jit(solution)/shard_map/all_gather | solution.py:36
  100.9 69.5 %copy-start = (f32[256]{0:T(256)S(1)}, f32[256]{0:T(256)}, u32[]{:S(2)}) copy-start(f32[256]{0:T(256)} %param.5) | copy-start | bytes 3076
Sparse Core Ops, SparseCore 0:
  10.4 160.0 all-gather.1
where the time goes:
time: 200 us
  blocking collectives  102 us (51%)
  waiting for transfers between devices  67.3 us (34%)
  between operations  14.1 us (7%)
  matrix products  11.3 us (6%)
  local copies, waits for them, and re-layouts  4.17 us (2%)
    all_gather x1, waiting for transfers between devices, per_device(): lax.all_gather(wave, 'band', axis=0, tiled=True)  66.7 us
    all_to_all x2, blocking collectives, copy_for_each(): lax.all_to_all(jnp.broadcast_to(value[None], (length, *value.shape)), axi...  54.1 us
    all_to_all x1, blocking collectives, per_device(): lax.all_to_all(ritz_rows, 'band', split_axis=1, concat_axis=0, tiled=True)  48.4 us
    dot_general x1, matrix products, per_device(): lax.dot_general(ritz_cols, lax.all_gather(wave, 'band', axis=0, tiled=Tru...  11.3 us
  transfers between devices with their start and end apart: 1, of which 1 were waited for; matrix products, arithmetic and copies ran while one was open for 2% of the time, Pallas kernels for 0%

commit v1 on v0

v1 whole, which is shorter than its diff:
```python
import jax
import jax.numpy as jnp
from jax import lax
from jax.experimental import pallas as pl
from jax.experimental.pallas import tpu as pltpu
from jax.sharding import PartitionSpec as P

NB = 4096
MESH = pl.DeviceIdType.MESH
F32, BF16 = jnp.float32, jnp.bfloat16

NK = 5
SLABS = 4

N_RINGS = 13


def at(x, y, z, core):
    return (x * 4 + (y // 2) * 2 + core, (y % 2) * 4 + z)


def kernel(
    wave, ritz, occ, out, dens,
    rt_src, stage, rt, w, cbuf, occ_rows, occ_cols, dpart, dsend, dslot,
    sa_send, sa_recv, s0_send, s0_recv, s1_send, s1_recv, ring_send, ring_recv,
    core_send, core_recv, occ_send, occ_recv, c_send, c_recv, d_send, d_recv,
):
    band, grid = lax.axis_index("band"), lax.axis_index("grid")
    x, yhi, c = band // 4, (band // 2) % 2, band % 2
    ylo, z = grid // 4, grid % 4
    y = yhi * 2 + ylo
    xj = 2 * ylo + z // 2
    zb = z % 2
    mine = yhi * 2 + c

    def half_of(yy):
        return (yy // 2 + yy % 2 + 1) % 2

    def send(src, dst, send_sem, recv_sem, device):
        return pltpu.make_async_remote_copy(
            src_ref=src, dst_ref=dst, send_sem=send_sem, recv_sem=recv_sem,
            device_id=device, device_id_type=MESH,
        )

    rt_src[...] = ritz[...].T.reshape(2, 4, 4, 16, 256)
    occ_rows[mine] = occ[...]

    def scatter(d):
        p = (z * 4 + y + d) % 16
        zp, yp = p // 4, p % 4
        return send(
            rt_src.at[:, zp, yp],
            stage.at[xj, pl.ds(zb * 2, 2), :, pl.ds(pl.multiple_of(yhi * 256, 256), 256)],
            s0_send.at[d], s0_recv.at[d], at(x, yp, zp, c),
        )

    def scatter_in(d):
        p = (z * 4 + y - d + 16) % 16
        zp, yp = p // 4, p % 4
        return send(
            rt_src.at[:, zp, yp],
            stage.at[2 * (yp % 2) + zp // 2, pl.ds((zp % 2) * 2, 2), :,
                     pl.ds(pl.multiple_of((yp // 2) * 256, 256), 256)],
            s0_send.at[d], s0_recv.at[d], at(x, yp, zp, c),
        )

    def wave_copy(k, j):
        up, core = j // 2, j % 2
        yy = (y + 1) % 4 if up else (y + 3) % 4
        col = pl.multiple_of(half_of(yy) * 1280 + core * 640 + k * 128, 128)
        return send(
            wave.at[:, pl.ds(col, 128)],
            w.at[k, c, pl.ds(pl.multiple_of(x * 512 + yhi * 256, 256), 256), :],
            sa_send.at[k, j], sa_recv.at[k], at(x, yy, z, core),
        )

    def wave_in(k):
        rows = w.at[k, :, pl.ds(pl.multiple_of(x * 512, 512), 512), :]
        return send(rows, rows, sa_send.at[k, 0], sa_recv.at[k], at(x, y, z, c))

    def ring(i):
        if i < 5:
            me, plus, minus = x, at((x + 1) % 4, y, z, c), at((x + 3) % 4, y, z, c)
            block = lambda v, h: w.at[i, h, pl.ds(pl.multiple_of(v * 512, 512), 512), :]
        elif i < 8:
            me, plus, minus = y, at(x, (y + 1) % 4, z, c), at(x, (y + 3) % 4, z, c)
            block = lambda v, h: rt.at[c, i - 5, z, v, :, pl.ds(h * 1024, 1024)]
        elif i < 11:
            me, plus, minus = z, at(x, y, (z + 1) % 4, c), at(x, y, (z + 3) % 4, c)
            block = lambda v, h: rt.at[c, i - 8, v, pl.ds(h * 2, 2)]
        elif i == 11:
            me, plus, minus = z, at(x, y, (z + 1) % 4, c), at(x, y, (z + 3) % 4, c)
            block = lambda v, h: rt.at[c, 3, v, y, :, pl.ds(h * 1024, 1024)]
        else:
            me, plus, minus = y, at(x, (y + 1) % 4, z, c), at(x, (y + 3) % 4, z, c)
            block = lambda v, h: rt.at[c, 3, pl.ds(h * 2, 2), v]

        def copy(j, v, h):
            ref = block((me + v) % 4, h)
            return send(ref, ref, ring_send.at[i, j], ring_recv.at[i, j], plus if j < 3 else minus)

        return copy

    def own(i):
        copy = ring(i)
        copy(0, 0, 0).start()
        copy(3, 0, 1).start()
        copy(1, 0, 1).start()
        copy(4, 0, 0).start()

    def relay(i):
        copy = ring(i)
        copy(0, 3, 0).wait_recv()
        copy(2, 3, 0).start()
        copy(3, 1, 1).wait_recv()
        copy(5, 1, 1).start()

    def finish(i):
        copy = ring(i)
        copy(1, 3, 1).wait_recv()
        copy(4, 1, 0).wait_recv()
        copy(2, 2, 0).wait_recv()
        copy(5, 2, 1).wait_recv()

    def drain(i):
        copy = ring(i)
        for j, v, h in ((0, 0, 0), (3, 0, 1), (1, 0, 1), (4, 0, 0), (2, 3, 0), (5, 1, 1)):
            copy(j, v, h).wait_send()

    def spread(d):
        to = (x + d) % 4
        return send(
            stage.at[to],
            rt.at[c, :, z, y, :, pl.ds(pl.multiple_of(x * 512, 512), 512)],
            s1_send.at[d], s1_recv.at[d], at(to, y, z, c),
        )

    def spread_in(d):
        src = (x - d + 4) % 4
        return send(
            stage.at[src],
            rt.at[c, :, z, y, :, pl.ds(pl.multiple_of(src * 512, 512), 512)],
            s1_send.at[d], s1_recv.at[d], at(src, y, z, c),
        )

    def to_partner(s):
        return send(rt.at[c, s], rt.at[c, s], core_send.at[s], core_recv.at[s], at(x, y, z, 1 - c))

    def from_partner(s):
        return send(rt.at[1 - c, s], rt.at[1 - c, s], core_send.at[s], core_recv.at[s], at(x, y, z, 1 - c))

    def occ_copy(d):
        yy = y if d == 0 else (y + 2) % 4
        cc = c if d == 1 else 1 - c
        return send(occ, occ_rows.at[mine], occ_send.at[d], occ_recv.at[d], at(x, yy, z, cc))

    def occ_in(d):
        hi = yhi if d == 0 else 1 - yhi
        cc = c if d == 1 else 1 - c
        return send(occ, occ_rows.at[hi * 2 + cc], occ_send.at[d], occ_recv.at[d], at(x, y, z, 1 - c))

    def result_copy(k, s):
        col = pl.multiple_of(half_of(y) * 1280 + c * 640 + k * 128, 128)
        return send(
            cbuf.at[k, s], out.at[:, pl.ds(col, 128)],
            c_send.at[k, s], c_recv.at[0], at(x, 2 * (s // 2) + 1 - ylo, z, s % 2),
        )

    def density_copy(d):
        return send(
            dsend, dslot.at[x * 4 + half_of(y) * 2 + c], d_send.at[d], d_recv.at[0],
            at(d // 4, 2 * ((d // 2) % 2) + 1 - ylo, z, d % 2),
        )

    for d in range(1, 16):
        scatter(d).start()
    for k in range(2):
        for j in range(4):
            wave_copy(k, j).start()
    for d in range(3):
        occ_copy(d).start()
    stage[xj, pl.ds(zb * 2, 2), :, pl.ds(pl.multiple_of(yhi * 256, 256), 256)] = rt_src[:, z, y]

    wave_in(0).wait_recv()
    own(0)
    for d in range(1, 16):
        scatter_in(d).wait_recv()
    for d in range(1, 4):
        spread(d).start()
    rt[c, :, z, y, :, pl.ds(pl.multiple_of(x * 512, 512), 512)] = stage[x]
    wave_in(1).wait_recv()
    own(1)
    for d in range(1, 4):
        spread_in(d).wait_recv()
    for i in (5, 6, 7, 11):
        own(i)
    for k in range(2, NK):
        for j in range(4):
            wave_copy(k, j).start()
    relay(0)
    for i in (5, 6, 7, 11):
        relay(i)
    for i in (5, 6, 7):
        finish(i)
        own(i + 3)
    finish(11)
    own(12)
    relay(1)
    wave_in(2).wait_recv()
    own(2)
    for d in range(3):
        occ_in(d).wait_recv()
    for s in range(SLABS):
        occ_cols[s] = jnp.broadcast_to(occ_rows[s][0:1, :], (128, 256)).T
    relay(8)
    wave_in(3).wait_recv()
    own(3)
    relay(12)
    relay(9)
    wave_in(4).wait_recv()
    own(4)
    relay(2)
    finish(8)
    to_partner(0).start()
    relay(10)
    relay(3)
    finish(9)
    to_partner(1).start()
    finish(12)
    to_partner(3).start()
    finish(10)
    to_partner(2).start()
    relay(4)
    for s in range(SLABS):
        from_partner(s).wait_recv()

    dpart[...] = jnp.zeros_like(dpart)
    for k in range(NK):
        finish(k)

        @pl.loop(0, SLABS)
        def _(s):
            summed = jnp.dot(
                rt[0, s].reshape(256, 2048), w[k, 0], preferred_element_type=F32
            ) + jnp.dot(rt[1, s].reshape(256, 2048), w[k, 1], preferred_element_type=F32)
            rounded = summed.astype(BF16)
            cbuf[k, s] = rounded
            values = rounded.astype(F32)
            terms = occ_cols[s] * values * values
            dpart[k] += terms.reshape(32, 8, 128).sum(axis=0)
            result_copy(k, s).start()

    dsend[...] = jnp.zeros_like(dsend)
    for k in range(NK):
        dsend[k : k + 1, :] = jnp.sum(dpart[k], axis=0, keepdims=True)
    for d in range(16):
        density_copy(d).start()

    for d in range(1, 16):
        scatter(d).wait_send()
    for k in range(NK):
        for j in range(4):
            wave_copy(k, j).wait_send()
    for d in range(1, 4):
        spread(d).wait_send()
    for i in range(N_RINGS):
        drain(i)
    for s in range(SLABS):
        to_partner(s).wait_send()
    for d in range(3):
        occ_copy(d).wait_send()

    send(dslot, dslot, d_send.at[0], d_recv.at[0], at(x, y, z, c)).wait_recv()
    for g in range(4):
        total = dslot[g] + dslot[4 + g] + dslot[8 + g] + dslot[12 + g]
        dens[g * NK : (g + 1) * NK, :] = total[:NK] * (1.0 / NB)

    send(out, out, c_send.at[0, 0], c_recv.at[0], at(x, y, z, c)).wait_recv()
    for k in range(NK):
        for s in range(SLABS):
            result_copy(k, s).wait_send()
    for d in range(16):
        density_copy(d).wait_send()


def per_device(wave, ritz, occupation):
    occ = jnp.broadcast_to(occupation.reshape(1, 256), (8, 256))
    dma = pltpu.SemaphoreType.DMA
    vmem = pl.BlockSpec(memory_space=pltpu.VMEM)
    anywhere = pl.BlockSpec(memory_space=pl.ANY)
    rotated, density = pl.pallas_call(
        kernel,
        out_shape=(
            jax.ShapeDtypeStruct((256, 2560), BF16),
            jax.ShapeDtypeStruct((20, 128), F32),
        ),
        in_specs=[anywhere, vmem, vmem],
        out_specs=(anywhere, vmem),
        scratch_shapes=[
            pltpu.VMEM((2, 4, 4, 16, 256), BF16),
            pltpu.VMEM((4, 4, 16, 512), BF16),
            pltpu.VMEM((2, 4, 4, 4, 16, 2048), BF16),
            pltpu.VMEM((NK, 2, 2048, 128), BF16),
            pltpu.VMEM((NK, 4, 256, 128), BF16),
            pltpu.VMEM((4, 8, 256), F32),
            pltpu.VMEM((4, 256, 128), F32),
            pltpu.VMEM((NK, 8, 128), F32),
            pltpu.VMEM((8, 128), F32),
            pltpu.VMEM((16, 8, 128), F32),
            dma((NK, 4)), dma((NK,)),
            dma((16,)), dma((16,)),
            dma((4,)), dma((4,)),
            dma((N_RINGS, 6)), dma((N_RINGS, 6)),
            dma((4,)), dma((4,)),
            dma((3,)), dma((3,)),
            dma((NK, 4)), dma((1,)),
            dma((16,)), dma((1,)),
        ],
        compiler_params=pltpu.CompilerParams(
            has_side_effects=True, vmem_limit_bytes=60 * 1024 * 1024
        ),
        name="rotate",
    )(wave, ritz, occ)
    return rotated, density.reshape(2560)


def solution(mesh):
    return jax.shard_map(
        per_device,
        mesh=mesh,
        in_specs=(P("band", "grid"), P("band", "grid"), P("band")),
        out_specs=(P("band", "grid"), P("grid")),
        check_vma=False,
    )
```

time: 200 us -> 108 us (0.54)
  Pallas kernels: 0 us -> 103 us
  blocking collectives: 102 us -> 0 us
  waiting for transfers between devices: 67.3 us -> 0 us
  between operations: 14.1 us -> 0.65 us
  matrix products: 11.3 us -> 0 us
    pallas_call x0 -> x1, Pallas kernels: none -> 103 us  [per_device(): pl.pallas_call(kernel, out_shape=(jax.ShapeDtypeStruct((256, 2560), BF16)...]
    all_to_all x3 -> x0, blocking collectives: 102 us -> none  [the longest x2 54.1 us: copy_for_each(): lax.all_to_all(jnp.broadcast_to(value[None], (length, *value.shape)), axi...]
    all_gather x1 -> x0, waiting for transfers between devices: 66.7 us -> none  [per_device(): lax.all_gather(wave, 'band', axis=0, tiled=True)]
    dot_general x1 -> x0, matrix products: 11.3 us -> none  [per_device(): lax.dot_general(ritz_cols, lax.all_gather(wave, 'band', axis=0, tiled=Tru...]
    all_to_all x1 -> x0, local copies, waits for them, and re-layouts: 2.86 us -> none  [per_device(): lax.all_to_all(ritz_rows, 'band', split_axis=1, concat_axis=0, tiled=True)]
  transfers between devices with their start and end apart: 1 -> 0, of which waited for: 1 -> 0; matrix products, arithmetic and copies ran while one was open for 2% -> 0% of each run, Pallas kernels for 0% -> 0%
where the time goes in v1:
time: 108 us
  Pallas kernels  103 us (95%)
  local copies, waits for them, and re-layouts  4.35 us (4%)
    pallas_call x1, Pallas kernels, per_device(): pl.pallas_call(kernel, out_shape=(jax.ShapeDtypeStruct((256, 2560), BF16)...  103 us
    unnamed x4, local copies, waits for them, and re-layouts  3.07 us

profile of v1, /device:TPU:1, one launch (start us, length us, event | category | flops | bytes accessed | tf_op | source)
XLA Modules:
  0.0 107.9 jit_solution(3036925375710916828)
XLA Ops:
  0.6 1.3 %broadcast_in_dim.2.occ = f32[8,256]{1,0:T(8,128)} broadcast(f32[256]{0:T(256)} %param.5), dimensions={1} | broadcast | bytes 9216 | tf_op jit(solution)/shard_map/broadcast_in_dim | solution.py:287
  1.9 102.9 %rotate.1 = (bf16[256,2560]{1,0:T(8,128)(2,1)}, f32[20,128]{1,0:T(8,128)}) custom-call(bf16[256,2560]{1,0:T(8,128)(2,1)} %wave.1, bf16[256,512]{1,0:T(8,128)(2,1)} %ritz.1, f32[8,256]{1,0:T(8,128)} %broadcast_in_dim.2.occ), custom_call_target="tpu_custom_call" | custom-call | tf_op jit(solution)/shard_map/rotate/pallas_call | solution.py:291
  104.8 0.0 copy-start
  104.8 2.5 %copy.7 = bf16[256,2560]{1,0:T(8,128)(2,1)} copy(bf16[256,2560]{1,0:T(8,128)(2,1)} %get-tuple-element.8) | data formatting | bytes 2621440
  107.3 0.0 copy-done
  107.3 0.6 copy.8
Async XLA Ops:
  104.8 2.5 %copy-start = (f32[20,128]{1,0:T(8,128)S(1)}, f32[20,128]{1,0:T(8,128)}, u32[]{:S(2)}) copy-start(f32[20,128]{1,0:T(8,128)} %get-tuple-element.5) | copy-start | bytes 30724

commit v2 on v1

--- a/solution.py
+++ b/solution.py
@@ -42,8 +42,22 @@
             device_id=device, device_id_type=MESH,
         )
 
-    rt_src[...] = ritz[...].T.reshape(2, 4, 4, 16, 256)
-    occ_rows[mine] = occ[...]
+    peers = [at(x, ((z * 4 + y + d) % 16) % 4, ((z * 4 + y + d) % 16) // 4, c) for d in range(1, 16)]
+    peers += [at((x + d) % 4, y, z, c) for d in range(1, 4)]
+    peers += [at(x, (y + d) % 4, z, 1 - c) for d in range(4)]
+    peers += [
+        at((x + d) % 4, (y + e) % 4, z, f) for d in range(1, 4) for e in (1, 3) for f in range(2)
+    ]
+    barrier = pltpu.get_barrier_semaphore()
+    with jax.named_scope("signal"):
+        for peer in peers:
+            pl.semaphore_signal(barrier, inc=1, device_id=peer, device_id_type=MESH)
+
+    with jax.named_scope("transpose"):
+        rt_src[...] = ritz[...].T.reshape(2, 4, 4, 16, 256)
+        occ_rows[mine] = jnp.broadcast_to(occ[...], (8, 256))
+    with jax.named_scope("barrier"):
+        pl.semaphore_wait(barrier, len(peers))
 
     def scatter(d):
         p = (z * 4 + y + d) % 16
@@ -64,24 +78,27 @@
             s0_send.at[d], s0_recv.at[d], at(x, yp, zp, c),
         )
 
+    def cells(k):
+        return pl.ds((k % 2) * 128, 128)
+
     def wave_copy(k, j):
         up, core = j // 2, j % 2
         yy = (y + 1) % 4 if up else (y + 3) % 4
         col = pl.multiple_of(half_of(yy) * 1280 + core * 640 + k * 128, 128)
         return send(
             wave.at[:, pl.ds(col, 128)],
-            w.at[k, c, pl.ds(pl.multiple_of(x * 512 + yhi * 256, 256), 256), :],
+            w.at[k // 2, c, pl.ds(pl.multiple_of(x * 512 + yhi * 256, 256), 256), cells(k)],
             sa_send.at[k, j], sa_recv.at[k], at(x, yy, z, core),
         )
 
     def wave_in(k):
-        rows = w.at[k, :, pl.ds(pl.multiple_of(x * 512, 512), 512), :]
+        rows = w.at[k // 2, :, pl.ds(pl.multiple_of(x * 512, 512), 512), cells(k)]
         return send(rows, rows, sa_send.at[k, 0], sa_recv.at[k], at(x, y, z, c))
 
     def ring(i):
         if i < 5:
             me, plus, minus = x, at((x + 1) % 4, y, z, c), at((x + 3) % 4, y, z, c)
-            block = lambda v, h: w.at[i, h, pl.ds(pl.multiple_of(v * 512, 512), 512), :]
+            block = lambda v, h: w.at[i // 2, h, pl.ds(pl.multiple_of(v * 512, 512), 512), cells(i)]
         elif i < 8:
             me, plus, minus = y, at(x, (y + 1) % 4, z, c), at(x, (y + 3) % 4, z, c)
             block = lambda v, h: rt.at[c, i - 5, z, v, :, pl.ds(h * 1024, 1024)]
@@ -152,12 +169,12 @@
     def occ_copy(d):
         yy = y if d == 0 else (y + 2) % 4
         cc = c if d == 1 else 1 - c
-        return send(occ, occ_rows.at[mine], occ_send.at[d], occ_recv.at[d], at(x, yy, z, cc))
+        return send(occ_rows.at[mine], occ_rows.at[mine], occ_send.at[d], occ_recv.at[d], at(x, yy, z, cc))
 
     def occ_in(d):
         hi = yhi if d == 0 else 1 - yhi
         cc = c if d == 1 else 1 - c
-        return send(occ, occ_rows.at[hi * 2 + cc], occ_send.at[d], occ_recv.at[d], at(x, y, z, 1 - c))
+        return send(occ_rows.at[mine], occ_rows.at[hi * 2 + cc], occ_send.at[d], occ_recv.at[d], at(x, y, z, 1 - c))
 
     def result_copy(k, s):
         col = pl.multiple_of(half_of(y) * 1280 + c * 640 + k * 128, 128)
@@ -172,119 +189,198 @@
             at(d // 4, 2 * ((d // 2) % 2) + 1 - ylo, z, d % 2),
         )
 
-    for d in range(1, 16):
-        scatter(d).start()
-    for k in range(2):
+    def send_wave(k):
         for j in range(4):
             wave_copy(k, j).start()
-    for d in range(3):
-        occ_copy(d).start()
-    stage[xj, pl.ds(zb * 2, 2), :, pl.ds(pl.multiple_of(yhi * 256, 256), 256)] = rt_src[:, z, y]
-
-    wave_in(0).wait_recv()
-    own(0)
-    for d in range(1, 16):
-        scatter_in(d).wait_recv()
-    for d in range(1, 4):
-        spread(d).start()
-    rt[c, :, z, y, :, pl.ds(pl.multiple_of(x * 512, 512), 512)] = stage[x]
-    wave_in(1).wait_recv()
-    own(1)
-    for d in range(1, 4):
-        spread_in(d).wait_recv()
-    for i in (5, 6, 7, 11):
-        own(i)
-    for k in range(2, NK):
-        for j in range(4):
-            wave_copy(k, j).start()
-    relay(0)
-    for i in (5, 6, 7, 11):
-        relay(i)
-    for i in (5, 6, 7):
-        finish(i)
-        own(i + 3)
-    finish(11)
-    own(12)
-    relay(1)
-    wave_in(2).wait_recv()
-    own(2)
-    for d in range(3):
-        occ_in(d).wait_recv()
-    for s in range(SLABS):
-        occ_cols[s] = jnp.broadcast_to(occ_rows[s][0:1, :], (128, 256)).T
-    relay(8)
-    wave_in(3).wait_recv()
-    own(3)
-    relay(12)
-    relay(9)
-    wave_in(4).wait_recv()
-    own(4)
-    relay(2)
-    finish(8)
-    to_partner(0).start()
-    relay(10)
-    relay(3)
-    finish(9)
-    to_partner(1).start()
-    finish(12)
-    to_partner(3).start()
-    finish(10)
-    to_partner(2).start()
-    relay(4)
-    for s in range(SLABS):
-        from_partner(s).wait_recv()
-
-    dpart[...] = jnp.zeros_like(dpart)
-    for k in range(NK):
-        finish(k)
-
+
+    def slab(v, s):
+        return rt[v, s].reshape(256, 2048)
+
+    def take(k, s, summed):
+        rounded = summed.astype(BF16)
+        cbuf[k, s] = rounded
+        values = rounded.astype(F32)
+        terms = occ_cols[s] * values * values
+        dpart[k] += terms.reshape(32, 8, 128).sum(axis=0)
+
+    def wide(pair, s):
+        summed = jnp.dot(slab(0, s), w[pair, 0], preferred_element_type=F32)
+        summed += jnp.dot(slab(1, s), w[pair, 1], preferred_element_type=F32)
+        for n in range(2):
+            take(2 * pair + n, s, summed[:, n * 128 : (n + 1) * 128])
+        for n in range(2):
+            result_copy(2 * pair + n, s).start()
+
+    def narrow(s):
+        summed = jnp.dot(slab(0, s), w[2, 0, :, :128], preferred_element_type=F32)
+        summed += jnp.dot(slab(1, s), w[2, 1, :, :128], preferred_element_type=F32)
+        take(4, s, summed)
+        result_copy(4, s).start()
+
+    def all_slabs(body):
         @pl.loop(0, SLABS)
-        def _(s):
-            summed = jnp.dot(
-                rt[0, s].reshape(256, 2048), w[k, 0], preferred_element_type=F32
-            ) + jnp.dot(rt[1, s].reshape(256, 2048), w[k, 1], preferred_element_type=F32)
-            rounded = summed.astype(BF16)
-            cbuf[k, s] = rounded
-            values = rounded.astype(F32)
-            terms = occ_cols[s] * values * values
-            dpart[k] += terms.reshape(32, 8, 128).sum(axis=0)
-            result_copy(k, s).start()
-
-    dsend[...] = jnp.zeros_like(dsend)
-    for k in range(NK):
-        dsend[k : k + 1, :] = jnp.sum(dpart[k], axis=0, keepdims=True)
-    for d in range(16):
-        density_copy(d).start()
-
-    for d in range(1, 16):
-        scatter(d).wait_send()
-    for k in range(NK):
-        for j in range(4):
-            wave_copy(k, j).wait_send()
-    for d in range(1, 4):
-        spread(d).wait_send()
-    for i in range(N_RINGS):
-        drain(i)
-    for s in range(SLABS):
-        to_partner(s).wait_send()
-    for d in range(3):
-        occ_copy(d).wait_send()
-
-    send(dslot, dslot, d_send.at[0], d_recv.at[0], at(x, y, z, c)).wait_recv()
-    for g in range(4):
-        total = dslot[g] + dslot[4 + g] + dslot[8 + g] + dslot[12 + g]
-        dens[g * NK : (g + 1) * NK, :] = total[:NK] * (1.0 / NB)
-
-    send(out, out, c_send.at[0, 0], c_recv.at[0], at(x, y, z, c)).wait_recv()
-    for k in range(NK):
+        def _(t):
+            body((t % 2) * 2 + t // 2)
+
+    with jax.named_scope("start"):
+        for d in range(1, 16):
+            scatter(d).start()
+        send_wave(0)
+        send_wave(1)
+        for d in range(3):
+            occ_copy(d).start()
+        stage[xj, pl.ds(zb * 2, 2), :, pl.ds(pl.multiple_of(yhi * 256, 256), 256)] = rt_src[:, z, y]
+    with jax.named_scope("scatter_in"):
+        for d in range(1, 16):
+            scatter_in(d).wait_recv()
+    with jax.named_scope("spread"):
+        for d in range(1, 4):
+            spread(d).start()
+        rt[c, :, z, y, :, pl.ds(pl.multiple_of(x * 512, 512), 512)] = stage[x]
+    with jax.named_scope("wave0"):
+        wave_in(0).wait_recv()
+        own(0)
+    with jax.named_scope("spread_in"):
+        for d in range(1, 4):
+            spread_in(d).wait_recv()
+        own(5)
+        own(6)
+        own(7)
+        own(11)
+        send_wave(2)
+    with jax.named_scope("wave1"):
+        wave_in(1).wait_recv()
+        own(1)
+    with jax.named_scope("occ"):
+        for d in range(3):
+            occ_in(d).wait_recv()
         for s in range(SLABS):
-            result_copy(k, s).wait_send()
-    for d in range(16):
-        density_copy(d).wait_send()
+            occ_cols[s] = jnp.broadcast_to(occ_rows[s][0:1, :], (128, 256)).T
+        dpart[...] = jnp.zeros_like(dpart)
+    with jax.named_scope("relay5"):
+        relay(5)
+        relay(6)
+        relay(7)
+        relay(11)
+    with jax.named_scope("finish5"):
+        finish(5)
+        own(8)
+    with jax.named_scope("finish6"):
+        finish(6)
+        own(9)
+    with jax.named_scope("finish11"):
+        finish(11)
+        own(12)
+    with jax.named_scope("relay0"):
+        relay(0)
+        send_wave(3)
+    with jax.named_scope("finish7"):
+        finish(7)
+    with jax.named_scope("wave2"):
+        wave_in(2).wait_recv()
+        own(2)
+    with jax.named_scope("relay8"):
+        relay(8)
+        own(10)
+    with jax.named_scope("relay12"):
+        relay(12)
+        send_wave(4)
+    with jax.named_scope("relay1"):
+        relay(1)
+    with jax.named_scope("wave3"):
+        wave_in(3).wait_recv()
+        own(3)
+    with jax.named_scope("relay9"):
+        relay(9)
+    with jax.named_scope("finish8"):
+        finish(8)
+        to_partner(0).start()
+    with jax.named_scope("finish12"):
+        finish(12)
+        to_partner(3).start()
+    with jax.named_scope("relay10"):
+        relay(10)
+    with jax.named_scope("relay2"):
+        relay(2)
+    with jax.named_scope("wave4"):
+        wave_in(4).wait_recv()
+        own(4)
+    with jax.named_scope("finish9"):
+        finish(9)
+        to_partner(1).start()
+    with jax.named_scope("finish0"):
+        finish(0)
+        finish(1)
+    with jax.named_scope("slab0"):
+        from_partner(0).wait_recv()
+        wide(0, 0)
+    with jax.named_scope("slab3"):
+        from_partner(3).wait_recv()
+        wide(0, 3)
+    with jax.named_scope("finish10"):
+        finish(10)
+        to_partner(2).start()
+    with jax.named_scope("relay3"):
+        relay(3)
+    with jax.named_scope("slab1"):
+        from_partner(1).wait_recv()
+        wide(0, 1)
+    with jax.named_scope("slab2"):
+        from_partner(2).wait_recv()
+        wide(0, 2)
+    with jax.named_scope("finish2"):
+        finish(2)
+    with jax.named_scope("finish3"):
+        finish(3)
+    with jax.named_scope("relay4"):
+        relay(4)
+    with jax.named_scope("pair1"):
+        all_slabs(lambda s: wide(1, s))
+    with jax.named_scope("finish4"):
+        finish(4)
+    with jax.named_scope("last"):
+        all_slabs(narrow)
+
+    with jax.named_scope("density"):
+        dsend[...] = jnp.zeros_like(dsend)
+        for k in range(NK):
+            dsend[k : k + 1, :] = jnp.sum(dpart[k], axis=0, keepdims=True)
+        for d in range(16):
+            density_copy(d).start()
+
+    with jax.named_scope("drain"):
+        for d in range(1, 16):
+            scatter(d).wait_send()
+        for k in range(NK):
+            for j in range(4):
+                wave_copy(k, j).wait_send()
+        for d in range(1, 4):
+            spread(d).wait_send()
+        for i in range(N_RINGS):
+            drain(i)
+        for s in range(SLABS):
+            to_partner(s).wait_send()
+        for d in range(3):
+            occ_copy(d).wait_send()
+
+    with jax.named_scope("density_in"):
+        send(dslot, dslot, d_send.at[0], d_recv.at[0], at(x, y, z, c)).wait_recv()
+        for g in range(4):
+            total = dslot[g] + dslot[4 + g] + dslot[8 + g] + dslot[12 + g]
+            dens[g * NK : (g + 1) * NK, :] = total[:NK] * (1.0 / NB)
+
+    with jax.named_scope("out_in"):
+        send(out, out, c_send.at[0, 0], c_recv.at[0], at(x, y, z, c)).wait_recv()
+    with jax.named_scope("out_sent"):
+        for k in range(NK):
+            for s in range(SLABS):
+                result_copy(k, s).wait_send()
+        for d in range(16):
+            density_copy(d).wait_send()
 
 
 def per_device(wave, ritz, occupation):
-    occ = jnp.broadcast_to(occupation.reshape(1, 256), (8, 256))
+    occ = occupation.reshape(1, 256)
     dma = pltpu.SemaphoreType.DMA
     vmem = pl.BlockSpec(memory_space=pltpu.VMEM)
     anywhere = pl.BlockSpec(memory_space=pl.ANY)
@@ -300,7 +396,7 @@
             pltpu.VMEM((2, 4, 4, 16, 256), BF16),
             pltpu.VMEM((4, 4, 16, 512), BF16),
             pltpu.VMEM((2, 4, 4, 4, 16, 2048), BF16),
-            pltpu.VMEM((NK, 2, 2048, 128), BF16),
+            pltpu.VMEM((3, 2, 2048, 256), BF16),
             pltpu.VMEM((NK, 4, 256, 128), BF16),
             pltpu.VMEM((4, 8, 256), F32),
             pltpu.VMEM((4, 256, 128), F32),
@@ -317,7 +413,7 @@
             dma((16,)), dma((1,)),
         ],
         compiler_params=pltpu.CompilerParams(
-            has_side_effects=True, vmem_limit_bytes=60 * 1024 * 1024
+            has_side_effects=True, collective_id=0, vmem_limit_bytes=60 * 1024 * 1024
         ),
         name="rotate",
     )(wave, ritz, occ)

time: 108 us -> 80.6 us (0.75)
  Pallas kernels: 103 us -> 76.7 us
  local copies, waits for them, and re-layouts: 4.35 us -> 3.07 us
    pallas_call x1, Pallas kernels: 103 us -> 76.7 us  [per_device(): pl.pallas_call(kernel, out_shape=(jax.ShapeDtypeStruct((256, 2560), BF16)...]
    broadcast_in_dim x1 -> x0, local copies, waits for them, and re-layouts: 1.28 us -> none  [per_device(): occ = jnp.broadcast_to(occupation.reshape(1, 256), (8, 256))]
where the time goes in v2:
time: 80.6 us; the launch traced here: 80.4 us
  Pallas kernels  76.7 us (95%)
  local copies, waits for them, and re-layouts  3.07 us (4%)
    pallas_call x1, Pallas kernels, per_device(): pl.pallas_call(kernel, out_shape=(jax.ShapeDtypeStruct((256, 2560), BF16)...  76.7 us
    unnamed x4, local copies, waits for them, and re-layouts  3.07 us

profile of v2, /device:TPU:1, one launch (start us, length us, event | category | flops | bytes accessed | tf_op | source)
XLA Modules:
  0.0 80.4 jit_solution(15135932100018503107)
XLA Ops:
  0.6 76.7 %rotate.1 = (bf16[256,2560]{1,0:T(8,128)(2,1)}, f32[20,128]{1,0:T(8,128)}) custom-call(bf16[256,2560]{1,0:T(8,128)(2,1)} %wave.1, bf16[256,512]{1,0:T(8,128)(2,1)} %ritz.1, f32[1,256]{1,0:T(1,128)} %bitcast.3), custom_call_target="tpu_custom_call" | custom-call | tf_op jit(solution)/shard_map/rotate/pallas_call | solution.py:387
  77.3 0.0 copy-start
  77.4 2.5 %copy.7 = bf16[256,2560]{1,0:T(8,128)(2,1)} copy(bf16[256,2560]{1,0:T(8,128)(2,1)} %get-tuple-element.8) | data formatting | bytes 2621440
  79.8 0.0 copy-done
  79.8 0.6 copy.8
Async XLA Ops:
  77.3 2.5 %copy-start = (f32[20,128]{1,0:T(8,128)S(1)}, f32[20,128]{1,0:T(8,128)}, u32[]{:S(2)}) copy-start(f32[20,128]{1,0:T(8,128)} %get-tuple-element.5) | copy-start | bytes 30724

commit v3 on v0

v3 whole, which is shorter than its diff:
```python
import jax
import jax.numpy as jnp
from jax import lax
from jax.experimental import pallas as pl
from jax.experimental.pallas import tpu as pltpu
from jax.sharding import PartitionSpec as P

NB = 4096
MESH = pl.DeviceIdType.MESH
F32, BF16 = jnp.float32, jnp.bfloat16

NK = 5
CA = 1536

N_RINGS = 16

PARTNER_WAVE, FAR_WAVE, SCATTER, SPREAD, RING_X, RING_YZ, CORE, OCC, RESULT, DENSITY, LOCAL = range(11)
OWN_RESULT = RING_X


def at(x, y, z, core):
    return (x * 4 + (y // 2) * 2 + core, (y % 2) * 4 + z)


def kernel(
    wave, ritz, occ, out, dens,
    rt_src, stage, rt, w, cbuf, occ_rows, occ_cols, dpart, dsend, dslot,
    out_sem, in_sem, wave_sem, ring_sem, half_sem,
):
    band, grid = lax.axis_index("band"), lax.axis_index("grid")
    x, yhi, c = band // 4, (band // 2) % 2, band % 2
    ylo, z = grid // 4, grid % 4
    y = yhi * 2 + ylo
    xj = 2 * ylo + z // 2
    zb = z % 2
    mine = yhi * 2 + c
    near, far = yhi, 1 - yhi

    def many(n, i):
        return pl.ds(pl.multiple_of(i * n, n), n)

    def send(src, dst, send_sem, recv_sem, device):
        return pltpu.make_async_remote_copy(
            src_ref=src, dst_ref=dst, send_sem=send_sem, recv_sem=recv_sem,
            device_id=device, device_id_type=MESH,
        )

    def cells(k):
        return pl.ds((k % 2) * 128, 128)

    def wave_local(p):
        width = 256 if p < 2 else 128
        col = pl.multiple_of(yhi * 1280 + c * 640 + p * 256, 128)
        return pltpu.make_async_copy(
            wave.at[:, pl.ds(col, width)],
            w.at[p, c, many(256, x * 2 + near), pl.ds(0, width)],
            in_sem.at[LOCAL],
        )

    def wave_partner(p):
        width = 256 if p < 2 else 128
        col = pl.multiple_of(yhi * 1280 + (1 - c) * 640 + p * 256, 128)
        return send(
            wave.at[:, pl.ds(col, width)],
            w.at[p, c, many(256, x * 2 + near), pl.ds(0, width)],
            out_sem.at[PARTNER_WAVE], in_sem.at[PARTNER_WAVE], at(x, y, z, 1 - c),
        )

    def wave_far(k, core):
        col = pl.multiple_of((1 - yhi) * 1280 + core * 640 + k * 128, 128)
        return send(
            wave.at[:, pl.ds(col, 128)],
            w.at[k // 2, c, many(256, x * 2 + near), cells(k)],
            out_sem.at[FAR_WAVE], wave_sem.at[k], at(x, (y + 2) % 4, z, core),
        )

    def wave_in(k):
        rows = w.at[k // 2, :, many(256, x * 2 + far), cells(k)]
        return send(rows, rows, out_sem.at[FAR_WAVE], wave_sem.at[k], at(x, (y + 2) % 4, z, c))

    def scatter(d, src):
        p = (z * 4 + y + (16 - d if src else d)) % 16
        zp, yp = p // 4, p % 4
        ys, zs = (yp, zp) if src else (y, z)
        return send(
            rt_src.at[:, zp, yp],
            stage.at[2 * (ys % 2) + zs // 2, many(2, zs % 2), :, many(256, ys // 2)],
            out_sem.at[SCATTER], in_sem.at[SCATTER], at(x, yp, zp, c),
        )

    def spread(d, src):
        other = (x + (4 - d if src else d)) % 4
        return send(
            stage.at[other], rt.at[c, :, z, y, :, many(512, other if src else x)],
            out_sem.at[SPREAD], in_sem.at[SPREAD], at(other, y, z, c),
        )

    def ring(i):
        if i < 10:
            k, rows = i % 5, (near if i < 5 else far)
            block = lambda v, h: w.at[k // 2, h, many(256, v * 2 + rows), cells(k)]
        elif i == 10:
            block = lambda v, h: rt.at[c, :, z, v, :, pl.ds(h * (CA // 2), CA // 2)]
        elif i == 11:
            n = (2048 - CA) // 2
            block = lambda v, h: rt.at[c, :, v, y, :, pl.ds(CA + h * n, n)]
        elif i < 14:
            block = lambda v, h: rt.at[c, pl.ds((i - 12) * 2, 2), v, pl.ds(h * 2, 2), :, pl.ds(0, CA)]
        else:
            n = 2048 - CA
            block = lambda v, h: rt.at[c, pl.ds((i - 14) * 2, 2), pl.ds(h * 2, 2), v, :, pl.ds(CA, n)]
        return block, i

    def ring_copy(i, j, v, h):
        if isinstance(i, tuple):
            half = i[1]
            block = lambda v, h: rt.at[c, many(2, half), v, pl.ds(h * 2, 2), :, pl.ds(0, CA)]
            axis, slot = "z", 12 + half
        else:
            block, slot = ring(i)
            axis = "x" if i < 10 else "z" if i in (11, 12, 13) else "y"
        to = 1 if j < 3 else 3
        if axis == "x":
            me, device = x, at((x + to) % 4, y, z, c)
        elif axis == "y":
            me, device = y, at(x, (y + to) % 4, z, c)
        else:
            me, device = z, at(x, y, (z + to) % 4, c)
        ref = block((me + v) % 4, h)
        sent = out_sem.at[RING_X if axis == "x" else RING_YZ]
        if j in (0, 3):
            got = ring_sem.at[slot, j // 3]
        elif axis == "x":
            got = half_sem.at[2 + max(slot % 5 - 1, 0)]
        else:
            got = ring_sem.at[slot, 2]
        return send(ref, ref, sent, got, device)

    def own(i):
        ring_copy(i, 0, 0, 0).start()
        ring_copy(i, 3, 0, 1).start()
        ring_copy(i, 1, 0, 1).start()
        ring_copy(i, 4, 0, 0).start()

    def relay(i):
        ring_copy(i, 0, 3, 0).wait_recv()
        ring_copy(i, 2, 3, 0).start()
        ring_copy(i, 3, 1, 1).wait_recv()
        ring_copy(i, 5, 1, 1).start()

    def bytes_in(ref, sem):
        send(ref, ref, out_sem.at[0], sem, at(x, y, z, 1 - c)).wait_recv()

    def bytes_out(ref, sem):
        send(ref, ref, sem, in_sem.at[0], at(x, y, z, 1 - c)).wait_send()

    def finish(i):
        if isinstance(i, tuple):
            bytes_in(rt.at[c, many(2, i[1]), pl.ds(0, 2), :, :, pl.ds(0, CA)], ring_sem.at[12 + i[1], 2])
        elif i == 10:
            bytes_in(rt.at[c, :, 0, pl.ds(0, 2), :, pl.ds(0, CA)], ring_sem.at[i, 2])
        elif i == 11:
            bytes_in(rt.at[c, :, pl.ds(0, 2), 0, :, pl.ds(CA, 2048 - CA)], ring_sem.at[i, 2])
        else:
            bytes_in(rt.at[c, pl.ds((i - 14) * 2, 2), :, pl.ds(0, 2), :, pl.ds(CA, 2048 - CA)], ring_sem.at[i, 2])

    def finish_wave(g):
        bytes_in(w.at[0, :, pl.ds(0, 512 if g else 1024), :], half_sem.at[2 + g])

    zfar, znear = (0, far), (0, near)

    def partner(half, part, src=False):
        cc = 1 - c if src else c
        cols = pl.ds(0, CA) if part == 0 else pl.ds(CA, 2048 - CA)
        ref = rt.at[cc, many(2, half), :, :, :, cols]
        return send(ref, ref, out_sem.at[CORE], half_sem.at[half], at(x, y, z, 1 - c))

    def occ_copy(d, src=False):
        yy = y if d == 0 else (y + 2) % 4
        cc = c if d == 1 else 1 - c
        row = (yy // 2) * 2 + cc if src else mine
        return send(
            occ_rows.at[mine], occ_rows.at[row], out_sem.at[OCC], in_sem.at[OCC], at(x, yy, z, cc)
        )

    def result(k, hi, core):
        return send(
            cbuf.at[k, hi * 2 + core], out.at[:, many(128, yhi * 10 + c * 5 + k)],
            out_sem.at[RESULT], in_sem.at[RESULT], at(x, hi * 2 + ylo, z, core),
        )

    def result_here(k):
        return pltpu.make_async_copy(
            cbuf.at[k, mine], out.at[:, many(128, yhi * 10 + c * 5 + k)], in_sem.at[OWN_RESULT]
        )

    def density_copy(d):
        to = at((x + d // 4) % 4, (y + 2 * ((d // 2) % 2)) % 4, z, (c + d) % 2)
        return send(dsend, dslot.at[band], out_sem.at[DENSITY], in_sem.at[DENSITY], to)

    def take(k, s, summed):
        rounded = summed.astype(BF16)
        cbuf[k, s] = rounded
        values = rounded.astype(F32)
        terms = occ_cols[s] * values * values
        dpart[k] += terms.reshape(32, 8, 128).sum(axis=0)

    def product(s, ks):
        cols = pl.ds((ks[0] % 2) * 128, 128 * len(ks))
        parts = [
            jnp.dot(
                rt[v, s].reshape(256, 2048), w[ks[0] // 2, v, :, cols], preferred_element_type=F32
            )
            for v in range(2)
        ]
        return parts[0] + parts[1]

    def blocks(ks, hi):
        @pl.loop(0, 2)
        def _(core):
            s = hi * 2 + core
            summed = product(s, ks)
            for n, k in enumerate(ks):
                take(k, s, summed[:, n * 128 : (n + 1) * 128])
            if hi is far:
                for k in ks:
                    result(k, hi, core).start()

        if hi is near:
            for k in ks:
                result(k, hi, 1 - c).start()
            for k in ks:
                result_here(k).start()

    with jax.named_scope("signal"):
        for p in range(3):
            wave_local(p).start()
        peers = []
        for d in range(1, 16):
            p = (z * 4 + y + d) % 16
            peers.append(at(x, p % 4, p // 4, c))
        for d in range(1, 16):
            if d != 2:
                peers.append(at((x + d // 4) % 4, (y + 2 * ((d // 2) % 2)) % 4, z, (c + d) % 2))
        barrier = pltpu.get_barrier_semaphore()
        for peer in peers:
            pl.semaphore_signal(barrier, inc=1, device_id=peer, device_id_type=MESH)

    with jax.named_scope("transpose"):
        rt_src[...] = ritz[...].T.reshape(2, 4, 4, 16, 256)
        occ_rows[mine] = jnp.broadcast_to(occ[...], (8, 256))
        stage[xj, many(2, zb), :, many(256, yhi)] = rt_src[:, z, y]
        dpart[...] = jnp.zeros_like(dpart)
        dsend[...] = jnp.zeros_like(dsend)
    with jax.named_scope("barrier"):
        pl.semaphore_wait(barrier, len(peers))

    with jax.named_scope("start"):
        for d in range(1, 16):
            scatter(d, 0).start()
        few = wave.at[:, pl.ds(0, 640)]
        pltpu.make_async_copy(few, few, in_sem.at[LOCAL]).wait()
        for p in range(3):
            wave_partner(p).start()
        for d in range(3):
            occ_copy(d).start()
    with jax.named_scope("pw"):
        bytes_in(wave.at[:, pl.ds(0, 640)], in_sem.at[PARTNER_WAVE])
        own(0)
    with jax.named_scope("scin"):
        bytes_in(w.at[0, 0, pl.ds(0, 480), :], in_sem.at[SCATTER])
        for d in range(1, 4):
            spread(d, 0).start()
        rt[c, :, z, y, :, many(512, x)] = stage[x]
        for core in range(2):
            wave_far(0, core).start()
        for core in range(2):
            wave_far(1, core).start()
        own(1)
        own(2)
        own(3)
    with jax.named_scope("spin"):
        bytes_in(stage.at[pl.ds(0, 3)], in_sem.at[SPREAD])
        own(10)
        own(11)
    with jax.named_scope("occ"):
        bytes_in(occ_rows.at[pl.ds(0, 3)], in_sem.at[OCC])
        for s in range(4):
            occ_cols[s] = jnp.broadcast_to(occ_rows[s][0:1, :], (128, 256)).T
    with jax.named_scope("s1relay"):
        relay(10)
        relay(11)
    with jax.named_scope("relay0"):
        relay(0)
    with jax.named_scope("wave0"):
        wave_in(0).wait_recv()
        own(5)
    with jax.named_scope("z1fin"):
        finish(11)
        own(14)
        own(15)
    with jax.named_scope("s1fin"):
        finish(10)
        own(zfar)
    with jax.named_scope("relay1"):
        relay(1)
    with jax.named_scope("y0relay"):
        relay(14)
    with jax.named_scope("relay2"):
        relay(2)
    with jax.named_scope("wave1"):
        wave_in(1).wait_recv()
        own(6)
    with jax.named_scope("y1relay"):
        relay(15)
        for core in range(2):
            wave_far(2, core).start()
    with jax.named_scope("relay3"):
        relay(3)
    with jax.named_scope("relay5"):
        relay(5)
    with jax.named_scope("zfrelay"):
        relay(zfar)
        own(znear)
        own(4)
    with jax.named_scope("y0fin"):
        finish(14)
        partner(0, 1).start()
        finish(15)
        partner(1, 1).start()
        for core in range(2):
            wave_far(3, core).start()
        for core in range(2):
            wave_far(4, core).start()
    with jax.named_scope("relay6"):
        relay(6)
    with jax.named_scope("wave2"):
        wave_in(2).wait_recv()
        own(7)
    with jax.named_scope("relay4"):
        relay(4)
    with jax.named_scope("zffin"):
        finish(zfar)
        partner(far, 0).start()
    with jax.named_scope("wave3"):
        wave_in(3).wait_recv()
        own(8)
    with jax.named_scope("relay7"):
        relay(7)
    with jax.named_scope("znrelay"):
        relay(znear)
    with jax.named_scope("wave4"):
        wave_in(4).wait_recv()
        own(9)
    with jax.named_scope("fw0"):
        finish_wave(0)
    with jax.named_scope("fromF"):
        bytes_in(rt.at[1 - c, many(2, far)], half_sem.at[far])
    with jax.named_scope("b01F"):
        blocks((0,1,), far)
    with jax.named_scope("relay8"):
        relay(8)
    with jax.named_scope("znfin"):
        finish(znear)
        partner(near, 0).start()
    with jax.named_scope("fw1"):
        finish_wave(1)
    with jax.named_scope("b2F"):
        blocks((2,), far)
    with jax.named_scope("relay9"):
        relay(9)
    with jax.named_scope("fromN"):
        bytes_in(rt.at[1 - c, many(2, near)], half_sem.at[near])
    with jax.named_scope("b01N"):
        blocks((0,1,), near)
    with jax.named_scope("fw2"):
        finish_wave(2)
    with jax.named_scope("b3F"):
        blocks((3,), far)
    with jax.named_scope("fw3"):
        finish_wave(3)
    with jax.named_scope("b4F"):
        blocks((4,), far)
    with jax.named_scope("b23N"):
        blocks((2,3,), near)
    with jax.named_scope("b4N"):
        blocks((4,), near)

    with jax.named_scope("density"):
        for k in range(NK):
            dsend[k : k + 1, :] = jnp.sum(dpart[k], axis=0, keepdims=True)
        dslot[band] = dsend[...]
        for d in range(1, 16):
            density_copy(d).start()

    with jax.named_scope("drain"):
        bytes_out(wave.at[:, pl.ds(0, 640)], out_sem.at[PARTNER_WAVE])
        bytes_out(wave.at[:, pl.ds(0, 1280)], out_sem.at[FAR_WAVE])
        bytes_out(w.at[0, 0, pl.ds(0, 480), :], out_sem.at[SCATTER])
        bytes_out(stage.at[pl.ds(0, 3)], out_sem.at[SPREAD])
        bytes_out(w.at[:, :, pl.ds(0, 1280), :], out_sem.at[RING_X])
        bytes_out(w.at[:, :, pl.ds(0, 1280), :], out_sem.at[RING_YZ])
        bytes_out(rt.at[c], out_sem.at[CORE])
        bytes_out(occ_rows.at[pl.ds(0, 3)], out_sem.at[OCC])

    with jax.named_scope("density_in"):
        bytes_in(dslot.at[pl.ds(0, 15)], in_sem.at[DENSITY])
        for g in range(4):
            total = dslot[g] + dslot[4 + g] + dslot[8 + g] + dslot[12 + g]
            dens[g * NK : (g + 1) * NK, :] = total[:NK] * (1.0 / NB)

    with jax.named_scope("out_in"):
        bytes_in(out.at[:, pl.ds(0, 1920)], in_sem.at[RESULT])
        few = out.at[:, pl.ds(0, 640)]
        pltpu.make_async_copy(few, few, in_sem.at[OWN_RESULT]).wait()
    with jax.named_scope("out_sent"):
        bytes_out(out.at[:, pl.ds(0, 1920)], out_sem.at[RESULT])
        bytes_out(dslot.at[pl.ds(0, 15)], out_sem.at[DENSITY])


def per_device(wave, ritz, occupation):
    occ = occupation.reshape(1, 256)
    dma = pltpu.SemaphoreType.DMA
    vmem = pl.BlockSpec(memory_space=pltpu.VMEM)
    anywhere = pl.BlockSpec(memory_space=pl.ANY)
    rotated, density = pl.pallas_call(
        kernel,
        out_shape=(
            jax.ShapeDtypeStruct((256, 2560), BF16),
            jax.ShapeDtypeStruct((20, 128), F32),
        ),
        in_specs=[anywhere, vmem, vmem],
        out_specs=(anywhere, vmem),
        scratch_shapes=[
            pltpu.VMEM((2, 4, 4, 16, 256), BF16),
            pltpu.VMEM((4, 4, 16, 512), BF16),
            pltpu.VMEM((2, 4, 4, 4, 16, 2048), BF16),
            pltpu.VMEM((3, 2, 2048, 256), BF16),
            pltpu.VMEM((NK, 4, 256, 128), BF16),
            pltpu.VMEM((4, 8, 256), F32),
            pltpu.VMEM((4, 256, 128), F32),
            pltpu.VMEM((NK, 8, 128), F32),
            pltpu.VMEM((8, 128), F32),
            pltpu.VMEM((16, 8, 128), F32),
            dma((11,)), dma((11,)), dma((NK,)), dma((N_RINGS, 3)), dma((6,)),
        ],
        compiler_params=pltpu.CompilerParams(
            has_side_effects=True, collective_id=0, vmem_limit_bytes=60 * 1024 * 1024
        ),
        name="rotate",
    )(wave, ritz, occ)
    return rotated, density.reshape(2560)


def solution(mesh):
    return jax.shard_map(
        per_device,
        mesh=mesh,
        in_specs=(P("band", "grid"), P("band", "grid"), P("band")),
        out_specs=(P("band", "grid"), P("grid")),
        check_vma=False,
    )
```

time: 200 us -> 76.8 us (0.38)
  blocking collectives: 102 us -> 0 us
  Pallas kernels: 0 us -> 72.3 us
  waiting for transfers between devices: 67.3 us -> 0 us
  between operations: 14.1 us -> 0.65 us
  matrix products: 11.3 us -> 0 us
    all_to_all x3 -> x0, blocking collectives: 102 us -> none  [the longest x2 54.1 us: copy_for_each(): lax.all_to_all(jnp.broadcast_to(value[None], (length, *value.shape)), axi...]
    pallas_call x0 -> x1, Pallas kernels: none -> 72.3 us  [per_device(): pl.pallas_call(kernel, out_shape=(jax.ShapeDtypeStruct((256, 2560), BF16)...]
    all_gather x1 -> x0, waiting for transfers between devices: 66.7 us -> none  [per_device(): lax.all_gather(wave, 'band', axis=0, tiled=True)]
    dot_general x1 -> x0, matrix products: 11.3 us -> none  [per_device(): lax.dot_general(ritz_cols, lax.all_gather(wave, 'band', axis=0, tiled=Tru...]
    all_to_all x1 -> x0, local copies, waits for them, and re-layouts: 2.86 us -> none  [per_device(): lax.all_to_all(ritz_rows, 'band', split_axis=1, concat_axis=0, tiled=True)]
  transfers between devices with their start and end apart: 1 -> 0, of which waited for: 1 -> 0; matrix products, arithmetic and copies ran while one was open for 2% -> 0% of each run, Pallas kernels for 0% -> 0%
where the time goes in v3:
time: 76.8 us; the launch traced here: 76.1 us
  Pallas kernels  72.3 us (94%)
  local copies, waits for them, and re-layouts  3.07 us (4%)
    pallas_call x1, Pallas kernels, per_device(): pl.pallas_call(kernel, out_shape=(jax.ShapeDtypeStruct((256, 2560), BF16)...  72.3 us
    unnamed x4, local copies, waits for them, and re-layouts  3.07 us

profile of v3, /device:TPU:1, one launch (start us, length us, event | category | flops | bytes accessed | tf_op | source)
XLA Modules:
  0.0 76.1 jit_solution(7224590215267665793)
XLA Ops:
  0.6 72.3 %rotate.1 = (bf16[256,2560]{1,0:T(8,128)(2,1)}, f32[20,128]{1,0:T(8,128)}) custom-call(bf16[256,2560]{1,0:T(8,128)(2,1)} %wave.1, bf16[256,512]{1,0:T(8,128)(2,1)} %ritz.1, f32[1,256]{1,0:T(1,128)} %bitcast.3), custom_call_target="tpu_custom_call" | custom-call | tf_op jit(solution)/shard_map/rotate/pallas_call | solution.py:426
  73.0 0.0 copy-start
  73.0 2.5 %copy.7 = bf16[256,2560]{1,0:T(8,128)(2,1)} copy(bf16[256,2560]{1,0:T(8,128)(2,1)} %get-tuple-element.8) | data formatting | bytes 2621440
  75.4 0.0 copy-done
  75.5 0.6 copy.8
Async XLA Ops:
  73.0 2.5 %copy-start = (f32[20,128]{1,0:T(8,128)S(1)}, f32[20,128]{1,0:T(8,128)}, u32[]{:S(2)}) copy-start(f32[20,128]{1,0:T(8,128)} %get-tuple-element.5) | copy-start | bytes 30724

commit v4 on v3

v4 whole, which is shorter than its diff:
```python
import jax
import jax.numpy as jnp
from jax import lax
from jax.experimental import pallas as pl
from jax.experimental.pallas import tpu as pltpu
from jax.sharding import PartitionSpec as P

NB = 4096
MESH = pl.DeviceIdType.MESH
F32, BF16 = jnp.float32, jnp.bfloat16

VM = 24 * 1024 * 1024
NK = 5
CA = 1536

N_RINGS = 18

PARTNER_WAVE, FAR_WAVE, SCATTER, SPREAD, RING_X, RING_YZ, CORE, OCC, RESULT, DENSITY, LOCAL = range(11)
OWN_RESULT, RITZ, OCC_HERE = RING_X, RING_YZ, CORE


def at(x, y, z, core):
    return (x * 4 + (y // 2) * 2 + core, (y % 2) * 4 + z)


def kernel(
    wave, ritz, occ, out, dens,
    ritz_here, occ_here, rt_src, stage, rt, w, cbuf, occ_rows, occ_cols, dpart, dsend, dslot,
    out_sem, in_sem, wave_sem, ring_sem, half_sem,
):
    band, grid = lax.axis_index("band"), lax.axis_index("grid")
    x, yhi, c = band // 4, (band // 2) % 2, band % 2
    ylo, z = grid // 4, grid % 4
    y = yhi * 2 + ylo
    xj = 2 * ylo + z // 2
    zb = z % 2
    mine = yhi * 2 + c
    near, far = yhi, 1 - yhi

    def many(n, i):
        return pl.ds(pl.multiple_of(i * n, n), n)

    def send(src, dst, send_sem, recv_sem, device):
        return pltpu.make_async_remote_copy(
            src_ref=src, dst_ref=dst, send_sem=send_sem, recv_sem=recv_sem,
            device_id=device, device_id_type=MESH,
        )

    def cells(k):
        return pl.ds(k * 128, 128)

    def wave_local():
        return pltpu.make_async_copy(
            wave.at[:, many(640, yhi * 2 + c)], w.at[c, many(256, x * 2 + near)], in_sem.at[LOCAL]
        )

    def wave_partner(p):
        first, n = ((0, 128), (128, 512))[p]
        col = pl.multiple_of((yhi * 2 + 1 - c) * 640 + first, 128)
        return send(
            wave.at[:, pl.ds(col, n)], w.at[c, many(256, x * 2 + near), pl.ds(first, n)],
            out_sem.at[PARTNER_WAVE], half_sem.at[1] if p else in_sem.at[PARTNER_WAVE],
            at(x, y, z, 1 - c),
        )

    def wave_far(k, core):
        col = pl.multiple_of((1 - yhi) * 1280 + core * 640 + k * 128, 128)
        return send(
            wave.at[:, pl.ds(col, 128)],
            w.at[c, many(256, x * 2 + near), cells(k)],
            out_sem.at[FAR_WAVE], wave_sem.at[k], at(x, (y + 2) % 4, z, core),
        )

    def wave_in(k):
        rows = w.at[:, many(256, x * 2 + far), cells(k)]
        return send(rows, rows, out_sem.at[FAR_WAVE], wave_sem.at[k], at(x, (y + 2) % 4, z, c))

    def scatter(d, src):
        p = (z * 4 + y + (16 - d if src else d)) % 16
        zp, yp = p // 4, p % 4
        ys, zs = (yp, zp) if src else (y, z)
        return send(
            rt_src.at[:, zp, yp],
            stage.at[2 * (ys % 2) + zs // 2, many(2, zs % 2), :, many(256, ys // 2)],
            out_sem.at[SCATTER], in_sem.at[SCATTER], at(x, yp, zp, c),
        )

    def spread(d, src):
        other = (x + (4 - d if src else d)) % 4
        return send(
            stage.at[other], rt.at[c, :, z, y, :, many(512, other if src else x)],
            out_sem.at[SPREAD], in_sem.at[SPREAD], at(other, y, z, c),
        )

    def ring(i):
        if i < 10:
            k, rows = i % 5, (near if i < 5 else far)
            block = lambda v, h: w.at[h, many(256, v * 2 + rows), cells(k)]
        elif i == 10:
            block = lambda v, h: rt.at[c, :, z, v, :, pl.ds(h * (CA // 2), CA // 2)]
        elif i == 11:
            n = (2048 - CA) // 2
            block = lambda v, h: rt.at[c, :, v, y, :, pl.ds(CA + h * n, n)]
        elif i < 16:
            block = lambda v, h: rt.at[c, pl.ds(h * 2, 2), v, (y + i - 12) % 4, :, pl.ds(0, CA)]
        else:
            n = 2048 - CA
            block = lambda v, h: rt.at[c, pl.ds((i - 16) * 2, 2), pl.ds(h * 2, 2), v, :, pl.ds(CA, n)]
        return block

    def ring_copy(i, j, v, h):
        block, slot = ring(i), i
        axis = "x" if i < 10 else "y" if i in (10, 16, 17) else "z"
        to = 1 if j < 3 else 3
        if axis == "x":
            me, device = x, at((x + to) % 4, y, z, c)
        elif axis == "y":
            me, device = y, at(x, (y + to) % 4, z, c)
        else:
            me, device = z, at(x, y, (z + to) % 4, c)
        ref = block((me + v) % 4, h)
        sent = out_sem.at[RING_X if axis == "x" else RING_YZ]
        if j in (0, 3):
            got = ring_sem.at[slot, j // 3]
        elif axis == "x":
            got = half_sem.at[2 + max(slot % 5 - 1, 0)]
        else:
            got = ring_sem.at[slot, 3 if slot == 10 and j in (2, 5) else 2]
        return send(ref, ref, sent, got, device)

    def own_first(i):
        ring_copy(i, 0, 0, 0).start()
        ring_copy(i, 3, 0, 1).start()

    def own_rest(i):
        ring_copy(i, 1, 0, 1).start()
        ring_copy(i, 4, 0, 0).start()

    def own(i):
        own_first(i)
        own_rest(i)

    def relay(i):
        ring_copy(i, 0, 3, 0).wait_recv()
        ring_copy(i, 2, 3, 0).start()
        ring_copy(i, 3, 1, 1).wait_recv()
        ring_copy(i, 5, 1, 1).start()

    def bytes_in(ref, sem):
        send(ref, ref, out_sem.at[0], sem, at(x, y, z, 1 - c)).wait_recv()

    def bytes_out(ref, sem):
        send(ref, ref, sem, in_sem.at[0], at(x, y, z, 1 - c)).wait_send()

    def finish(i, part=0):
        low, high = pl.ds(0, CA), pl.ds(CA, 2048 - CA)
        if i == 10:
            bytes_in(rt.at[c, :, 0, 0, :, low], ring_sem.at[i, 2 + part])
        elif i == 11:
            bytes_in(rt.at[c, :, pl.ds(0, 2), 0, :, high], ring_sem.at[i, 2])
        elif i < 16:
            bytes_in(rt.at[c, :, pl.ds(0, 2), 0, :, low], ring_sem.at[i, 2])
        else:
            bytes_in(rt.at[c, pl.ds(0, 2), :, pl.ds(0, 2), :, high], ring_sem.at[i, 2])

    def finish_wave(g):
        bytes_in(rt.at[0, 0, pl.ds(0, 2 if g else 4)], half_sem.at[2 + g])

    def partner(p):
        if p < 4:
            ref = rt.at[c, :, :, (y + p) % 4, :, pl.ds(0, CA)]
        else:
            ref = rt.at[c, pl.ds((p - 4) * 2, 2), :, :, :, pl.ds(CA, 2048 - CA)]
        return send(ref, ref, out_sem.at[CORE], half_sem.at[0], at(x, y, z, 1 - c))

    def occ_copy(d, src=False):
        yy = y if d == 0 else (y + 2) % 4
        cc = c if d == 1 else 1 - c
        row = (yy // 2) * 2 + cc if src else mine
        return send(
            occ_rows.at[mine], occ_rows.at[row], out_sem.at[OCC], in_sem.at[OCC], at(x, yy, z, cc)
        )

    def result(k, hi, core):
        return send(
            cbuf.at[k, hi * 2 + core], out.at[:, many(128, yhi * 10 + c * 5 + k)],
            out_sem.at[RESULT], in_sem.at[RESULT], at(x, hi * 2 + ylo, z, core),
        )

    def result_here(k):
        return pltpu.make_async_copy(
            cbuf.at[k, mine], out.at[:, many(128, yhi * 10 + c * 5 + k)], in_sem.at[OWN_RESULT]
        )

    def density_copy(d):
        to = at((x + d // 4) % 4, (y + 2 * ((d // 2) % 2)) % 4, z, (c + d) % 2)
        return send(dsend, dslot.at[band], out_sem.at[DENSITY], in_sem.at[DENSITY], to)

    def take(k, s, summed):
        rounded = summed.astype(BF16)
        cbuf[k, s] = rounded
        values = rounded.astype(F32)
        terms = occ_cols[s] * values * values
        dpart[k] += terms.reshape(32, 8, 128).sum(axis=0)

    def product(s, ks):
        cols = pl.ds(ks[0] * 128, 128 * len(ks))
        parts = [
            jnp.dot(
                rt[v, s].reshape(256, 2048), w[v, :, cols], preferred_element_type=F32
            )
            for v in range(2)
        ]
        return parts[0] + parts[1]

    def blocks(ks, hi):
        @pl.loop(0, 2)
        def _(core):
            s = hi * 2 + core
            summed = product(s, ks)
            for n, k in enumerate(ks):
                take(k, s, summed[:, n * 128 : (n + 1) * 128])
            if hi is far:
                for k in ks:
                    result(k, hi, core).start()

        if hi is near:
            for k in ks:
                result(k, hi, 1 - c).start()
            for k in ks:
                result_here(k).start()

    with jax.named_scope("signal"):
        load_ritz = pltpu.make_async_copy(ritz, ritz_here, in_sem.at[RITZ])
        load_occ = pltpu.make_async_copy(occ, occ_here, in_sem.at[OCC_HERE])
        load_ritz.start()
        load_occ.start()
        wave_local().start()
        peers = []
        for d in range(1, 16):
            p = (z * 4 + y + d) % 16
            peers.append(at(x, p % 4, p // 4, c))
        for d in range(1, 16):
            if d != 2:
                peers.append(at((x + d // 4) % 4, (y + 2 * ((d // 2) % 2)) % 4, z, (c + d) % 2))
        barrier = pltpu.get_barrier_semaphore()
        for peer in peers:
            pl.semaphore_signal(barrier, inc=1, device_id=peer, device_id_type=MESH)

    with jax.named_scope("transpose"):
        load_ritz.wait()
        load_occ.wait()
        rt_src[...] = ritz_here[...].T.reshape(2, 4, 4, 16, 256)
        occ_rows[mine] = jnp.broadcast_to(occ_here[...], (8, 256))
        stage[xj, many(2, zb), :, many(256, yhi)] = rt_src[:, z, y]
        dpart[...] = jnp.zeros_like(dpart)
        dsend[...] = jnp.zeros_like(dsend)
    with jax.named_scope("barrier"):
        pl.semaphore_wait(barrier, len(peers))

    with jax.named_scope("start"):
        for d in range(1, 16):
            scatter(d, 0).start()
        wave_local().wait()
        for p in range(2):
            wave_partner(p).start()
        for d in range(3):
            occ_copy(d).start()
    with jax.named_scope("pw"):
        bytes_in(wave.at[:, pl.ds(0, 128)], in_sem.at[PARTNER_WAVE])
        own(0)
        bytes_in(wave.at[:, pl.ds(0, 512)], half_sem.at[1])
        own_first(1)
    with jax.named_scope("scin"):
        bytes_in(w.at[0, pl.ds(0, 192)], in_sem.at[SCATTER])
        for d in range(1, 4):
            spread(d, 0).start()
        rt[c, :, z, y, :, many(512, x)] = stage[x]
        for core in range(2):
            wave_far(0, core).start()
        for core in range(2):
            wave_far(1, core).start()
        own_rest(1)
        own(2)
        own(3)
        own(4)
    with jax.named_scope("spin"):
        bytes_in(stage.at[pl.ds(0, 3)], in_sem.at[SPREAD])
        own(10)
        own(11)
        own(12)
    with jax.named_scope("occ"):
        bytes_in(occ_rows.at[pl.ds(0, 3)], in_sem.at[OCC])
        for s in range(4):
            occ_cols[s] = jnp.broadcast_to(occ_rows[s][0:1, :], (128, 256)).T
    with jax.named_scope("s1relay"):
        relay(10)
        relay(11)
    with jax.named_scope("relay0"):
        relay(0)
    with jax.named_scope("wave0"):
        wave_in(0).wait_recv()
        own(5)
    with jax.named_scope("finA"):
        finish(10, 0)
        own(13)
        own(15)
    with jax.named_scope("z1fin"):
        finish(11)
        own(16)
        own(17)
    with jax.named_scope("p0relay"):
        relay(12)
    with jax.named_scope("s1fin"):
        finish(10, 1)
        own(14)
    with jax.named_scope("relay1"):
        relay(1)
    with jax.named_scope("y0relay"):
        relay(16)
    with jax.named_scope("relay2"):
        relay(2)
    with jax.named_scope("wave1"):
        wave_in(1).wait_recv()
        own(6)
    with jax.named_scope("y1relay"):
        relay(17)
        for core in range(2):
            wave_far(2, core).start()
    with jax.named_scope("relay3"):
        relay(3)
    with jax.named_scope("relay5"):
        relay(5)
    with jax.named_scope("p1relay"):
        relay(13)
    with jax.named_scope("p0fin"):
        finish(12)
        partner(0).start()
    with jax.named_scope("p3relay"):
        relay(15)
    with jax.named_scope("relay4"):
        relay(4)
    with jax.named_scope("y0fin"):
        finish(16)
        partner(4).start()
        finish(17)
        partner(5).start()
        for core in range(2):
            wave_far(3, core).start()
        for core in range(2):
            wave_far(4, core).start()
    with jax.named_scope("p2relay"):
        relay(14)
    with jax.named_scope("relay6"):
        relay(6)
    with jax.named_scope("wave2"):
        wave_in(2).wait_recv()
        own(7)
    with jax.named_scope("p1fin"):
        finish(13)
        partner(1).start()
    with jax.named_scope("p3fin"):
        finish(15)
        partner(3).start()
    with jax.named_scope("wave3"):
        wave_in(3).wait_recv()
        own(8)
    with jax.named_scope("relay7"):
        relay(7)
    with jax.named_scope("p2fin"):
        finish(14)
        partner(2).start()
    with jax.named_scope("wave4"):
        wave_in(4).wait_recv()
        own(9)
    with jax.named_scope("fw0"):
        finish_wave(0)
    with jax.named_scope("from"):
        bytes_in(rt.at[1 - c], half_sem.at[0])
    with jax.named_scope("b01F"):
        blocks((0,1,), far)
    with jax.named_scope("relay8"):
        relay(8)
    with jax.named_scope("b01N"):
        blocks((0,1,), near)
    with jax.named_scope("relay9"):
        relay(9)
    with jax.named_scope("fw1"):
        finish_wave(1)
    with jax.named_scope("b2F"):
        blocks((2,), far)
    with jax.named_scope("b2N"):
        blocks((2,), near)
    with jax.named_scope("fw2"):
        finish_wave(2)
    with jax.named_scope("b3F"):
        blocks((3,), far)
    with jax.named_scope("fw3"):
        finish_wave(3)
    with jax.named_scope("b4F"):
        blocks((4,), far)
    with jax.named_scope("b34N"):
        blocks((3,4,), near)

    with jax.named_scope("density"):
        for k in range(NK):
            dsend[k : k + 1, :] = jnp.sum(dpart[k], axis=0, keepdims=True)
        dslot[band] = dsend[...]
        for d in range(1, 16):
            density_copy(d).start()

    with jax.named_scope("drain"):
        bytes_out(wave.at[:, pl.ds(0, 640)], out_sem.at[PARTNER_WAVE])
        bytes_out(wave.at[:, pl.ds(0, 1280)], out_sem.at[FAR_WAVE])
        bytes_out(w.at[0, pl.ds(0, 192)], out_sem.at[SCATTER])
        bytes_out(stage.at[pl.ds(0, 3)], out_sem.at[SPREAD])
        bytes_out(w.at[:, pl.ds(0, 1536)], out_sem.at[RING_X])
        bytes_out(w.at[:, pl.ds(0, 1536)], out_sem.at[RING_YZ])
        bytes_out(rt.at[c], out_sem.at[CORE])
        bytes_out(occ_rows.at[pl.ds(0, 3)], out_sem.at[OCC])

    with jax.named_scope("density_in"):
        bytes_in(dslot.at[pl.ds(0, 15)], in_sem.at[DENSITY])
        for g in range(4):
            total = dslot[g] + dslot[4 + g] + dslot[8 + g] + dslot[12 + g]
            dens[g * NK : (g + 1) * NK, :] = total[:NK] * (1.0 / NB)

    with jax.named_scope("out_in"):
        bytes_in(out.at[:, pl.ds(0, 1920)], in_sem.at[RESULT])
        few = out.at[:, pl.ds(0, 640)]
        pltpu.make_async_copy(few, few, in_sem.at[OWN_RESULT]).wait()
    with jax.named_scope("out_sent"):
        bytes_out(out.at[:, pl.ds(0, 1920)], out_sem.at[RESULT])
        bytes_out(dslot.at[pl.ds(0, 15)], out_sem.at[DENSITY])


def per_device(wave, ritz, occupation):
    wave, ritz, occ = (
        pltpu.with_memory_space_constraint(a, pltpu.HBM)
        for a in (wave, ritz, occupation.reshape(1, 256))
    )
    dma = pltpu.SemaphoreType.DMA
    vmem = pl.BlockSpec(memory_space=pltpu.VMEM)
    anywhere = pl.BlockSpec(memory_space=pl.ANY)
    rotated, density = pl.pallas_call(
        kernel,
        out_shape=(
            jax.ShapeDtypeStruct((256, 2560), BF16),
            jax.ShapeDtypeStruct((20, 128), F32),
        ),
        in_specs=[pl.BlockSpec(memory_space=pltpu.HBM)] * 3,
        out_specs=(anywhere, vmem),
        scratch_shapes=[
            pltpu.VMEM((256, 512), BF16),
            pltpu.VMEM((1, 256), F32),
            pltpu.VMEM((2, 4, 4, 16, 256), BF16),
            pltpu.VMEM((4, 4, 16, 512), BF16),
            pltpu.VMEM((2, 4, 4, 4, 16, 2048), BF16),
            pltpu.VMEM((2, 2048, 640), BF16),
            pltpu.VMEM((NK, 4, 256, 128), BF16),
            pltpu.VMEM((4, 8, 256), F32),
            pltpu.VMEM((4, 256, 128), F32),
            pltpu.VMEM((NK, 8, 128), F32),
            pltpu.VMEM((8, 128), F32),
            pltpu.VMEM((16, 8, 128), F32),
            dma((11,)), dma((11,)), dma((NK,)), dma((N_RINGS, 4)), dma((6,)),
        ],
        compiler_params=pltpu.CompilerParams(
            has_side_effects=True, collective_id=0, vmem_limit_bytes=VM
        ),
        name="rotate",
    )(wave, ritz, occ)
    return rotated, density.reshape(2560)


def solution(mesh):
    return jax.shard_map(
        per_device,
        mesh=mesh,
        in_specs=(P("band", "grid"), P("band", "grid"), P("band")),
        out_specs=(P("band", "grid"), P("grid")),
        check_vma=False,
    )
```

time: 76.8 us -> 72.5 us (0.944)
  Pallas kernels: 72.3 us -> 70 us
  local copies, waits for them, and re-layouts: 3.07 us -> 1.66 us
    pallas_call x1, Pallas kernels: 72.3 us -> 70 us  [per_device(): pl.pallas_call(kernel, out_shape=(jax.ShapeDtypeStruct((256, 2560), BF16)...]
    unnamed x4 -> x2, local copies, waits for them, and re-layouts: 3.07 us -> 1.66 us
where the time goes in v4:
time: 72.5 us; the launch traced here: 72.3 us
  Pallas kernels  70 us (97%)
  local copies, waits for them, and re-layouts  1.66 us (2%)
    pallas_call x1, Pallas kernels, per_device(): pl.pallas_call(kernel, out_shape=(jax.ShapeDtypeStruct((256, 2560), BF16)...  70 us
    unnamed x2, local copies, waits for them, and re-layouts  1.66 us

profile of v4, /device:TPU:1, one launch (start us, length us, event | category | flops | bytes accessed | tf_op | source)
XLA Modules:
  0.0 72.3 jit_solution(17225668559291229658)
XLA Ops:
  0.6 70.0 %rotate.1 = (bf16[256,2560]{1,0:T(8,128)(2,1)S(1)}, f32[20,128]{1,0:T(8,128)S(1)}) custom-call(bf16[256,2560]{1,0:T(8,128)(2,1)} %wave.1, bf16[256,512]{1,0:T(8,128)(2,1)} %ritz.1, f32[1,256]{1,0:T(1,128)} %bitcast.3), custom_call_target="tpu_custom_call" | custom-call | tf_op jit(solution)/shard_map/rotate/pallas_call | solution.py:445
  70.7 1.1 %copy.7 = bf16[256,2560]{1,0:T(8,128)(2,1)} copy(bf16[256,2560]{1,0:T(8,128)(2,1)S(1)} %get-tuple-element.8) | data formatting | bytes 2621440
  71.7 0.6 copy.8

commit v5 on v4

--- a/solution.py
+++ b/solution.py
@@ -11,12 +11,17 @@
 
 VM = 24 * 1024 * 1024
 NK = 5
-CA = 1536
+CA = 1408
 
 N_RINGS = 18
 
 PARTNER_WAVE, FAR_WAVE, SCATTER, SPREAD, RING_X, RING_YZ, CORE, OCC, RESULT, DENSITY, LOCAL = range(11)
 OWN_RESULT, RITZ, OCC_HERE = RING_X, RING_YZ, CORE
+
+IN_PLANE = sorted(
+    ((dy, dz) for dy in range(4) for dz in range(4) if dy or dz),
+    key=lambda d: -min(d[0], 4 - d[0]) - min(d[1], 4 - d[1]),
+)
 
 
 def at(x, y, z, core):
@@ -75,20 +80,18 @@
         rows = w.at[:, many(256, x * 2 + far), cells(k)]
         return send(rows, rows, out_sem.at[FAR_WAVE], wave_sem.at[k], at(x, (y + 2) % 4, z, c))
 
-    def scatter(d, src):
-        p = (z * 4 + y + (16 - d if src else d)) % 16
-        zp, yp = p // 4, p % 4
-        ys, zs = (yp, zp) if src else (y, z)
+    def scatter(dy, dz):
+        yp, zp = (y + dy) % 4, (z + dz) % 4
         return send(
             rt_src.at[:, zp, yp],
-            stage.at[2 * (ys % 2) + zs // 2, many(2, zs % 2), :, many(256, ys // 2)],
+            stage.at[xj, many(2, zb), :, many(256, yhi)],
             out_sem.at[SCATTER], in_sem.at[SCATTER], at(x, yp, zp, c),
         )
 
-    def spread(d, src):
-        other = (x + (4 - d if src else d)) % 4
+    def spread(d):
+        other = (x + d) % 4
         return send(
-            stage.at[other], rt.at[c, :, z, y, :, many(512, other if src else x)],
+            stage.at[other], rt.at[c, :, z, y, :, many(512, x)],
             out_sem.at[SPREAD], in_sem.at[SPREAD], at(other, y, z, c),
         )
 
@@ -97,16 +100,20 @@
             k, rows = i % 5, (near if i < 5 else far)
             block = lambda v, h: w.at[h, many(256, v * 2 + rows), cells(k)]
         elif i == 10:
-            block = lambda v, h: rt.at[c, :, z, v, :, pl.ds(h * (CA // 2), CA // 2)]
+            block = lambda v, h: rt.at[c, pl.ds(h * 2, 2), z, v, :, pl.ds(0, CA)]
         elif i == 11:
-            n = (2048 - CA) // 2
-            block = lambda v, h: rt.at[c, :, v, y, :, pl.ds(CA + h * n, n)]
+            block = lambda v, h: rt.at[c, pl.ds(h * 2, 2), v, y, :, pl.ds(CA, 2048 - CA)]
         elif i < 16:
             block = lambda v, h: rt.at[c, pl.ds(h * 2, 2), v, (y + i - 12) % 4, :, pl.ds(0, CA)]
         else:
             n = 2048 - CA
             block = lambda v, h: rt.at[c, pl.ds((i - 16) * 2, 2), pl.ds(h * 2, 2), v, :, pl.ds(CA, n)]
         return block
+
+    def sem_of(i, n):
+        if n == 3:
+            return 44 + (i == 14)
+        return i * 2 + n if i < 10 else 20 + (i - 10) * 3 + n
 
     def ring_copy(i, j, v, h):
         block, slot = ring(i), i
@@ -121,11 +128,11 @@
         ref = block((me + v) % 4, h)
         sent = out_sem.at[RING_X if axis == "x" else RING_YZ]
         if j in (0, 3):
-            got = ring_sem.at[slot, j // 3]
+            got = ring_sem.at[sem_of(slot, j // 3)]
         elif axis == "x":
             got = half_sem.at[2 + max(slot % 5 - 1, 0)]
         else:
-            got = ring_sem.at[slot, 3 if slot == 10 and j in (2, 5) else 2]
+            got = ring_sem.at[sem_of(slot, 3 if slot in (10, 14) and j in (2, 5) else 2)]
         return send(ref, ref, sent, got, device)
 
     def own_first(i):
@@ -154,24 +161,32 @@
 
     def finish(i, part=0):
         low, high = pl.ds(0, CA), pl.ds(CA, 2048 - CA)
-        if i == 10:
-            bytes_in(rt.at[c, :, 0, 0, :, low], ring_sem.at[i, 2 + part])
+        if i in (10, 14):
+            bytes_in(rt.at[c, :, 0, 0, :, low], ring_sem.at[sem_of(i, 2 + part)])
         elif i == 11:
-            bytes_in(rt.at[c, :, pl.ds(0, 2), 0, :, high], ring_sem.at[i, 2])
+            bytes_in(rt.at[c, :, pl.ds(0, 2), 0, :, high], ring_sem.at[sem_of(i, 2)])
         elif i < 16:
-            bytes_in(rt.at[c, :, pl.ds(0, 2), 0, :, low], ring_sem.at[i, 2])
+            bytes_in(rt.at[c, :, pl.ds(0, 2), 0, :, low], ring_sem.at[sem_of(i, 2)])
         else:
-            bytes_in(rt.at[c, pl.ds(0, 2), :, pl.ds(0, 2), :, high], ring_sem.at[i, 2])
+            bytes_in(rt.at[c, pl.ds(0, 2), :, pl.ds(0, 2), :, high], ring_sem.at[sem_of(i, 2)])
 
     def finish_wave(g):
         bytes_in(rt.at[0, 0, pl.ds(0, 2 if g else 4)], half_sem.at[2 + g])
 
-    def partner(p):
-        if p < 4:
-            ref = rt.at[c, :, :, (y + p) % 4, :, pl.ds(0, CA)]
+    def partner(p, vs=()):
+        if p == 2:
+            refs = [rt.at[c, :, (z + v) % 4, (y + 2) % 4, :, pl.ds(0, CA)] for v in vs]
+        elif p < 4:
+            refs = [rt.at[c, :, :, (y + p) % 4, :, pl.ds(0, CA)]]
+        elif p == 4:
+            refs = [rt.at[c, :, :, y, :, pl.ds(CA, 2048 - CA)]]
         else:
-            ref = rt.at[c, pl.ds((p - 4) * 2, 2), :, :, :, pl.ds(CA, 2048 - CA)]
-        return send(ref, ref, out_sem.at[CORE], half_sem.at[0], at(x, y, z, 1 - c))
+            refs = [
+                rt.at[c, pl.ds((p - 5) * 2, 2), :, (y + d) % 4, :, pl.ds(CA, 2048 - CA)]
+                for d in range(1, 4)
+            ]
+        for ref in refs:
+            send(ref, ref, out_sem.at[CORE], half_sem.at[0], at(x, y, z, 1 - c)).start()
 
     def occ_copy(d, src=False):
         yy = y if d == 0 else (y + 2) % 4
@@ -237,9 +252,8 @@
         load_occ.start()
         wave_local().start()
         peers = []
-        for d in range(1, 16):
-            p = (z * 4 + y + d) % 16
-            peers.append(at(x, p % 4, p // 4, c))
+        for dy, dz in IN_PLANE:
+            peers.append(at(x, (y + dy) % 4, (z + dz) % 4, c))
         for d in range(1, 16):
             if d != 2:
                 peers.append(at((x + d // 4) % 4, (y + 2 * ((d // 2) % 2)) % 4, z, (c + d) % 2))
@@ -259,8 +273,8 @@
         pl.semaphore_wait(barrier, len(peers))
 
     with jax.named_scope("start"):
-        for d in range(1, 16):
-            scatter(d, 0).start()
+        for dy, dz in IN_PLANE:
+            scatter(dy, dz).start()
         wave_local().wait()
         for p in range(2):
             wave_partner(p).start()
@@ -273,8 +287,8 @@
         own_first(1)
     with jax.named_scope("scin"):
         bytes_in(w.at[0, pl.ds(0, 192)], in_sem.at[SCATTER])
-        for d in range(1, 4):
-            spread(d, 0).start()
+        for d in (2, 1, 3):
+            spread(d).start()
         rt[c, :, z, y, :, many(512, x)] = stage[x]
         for core in range(2):
             wave_far(0, core).start()
@@ -296,6 +310,8 @@
     with jax.named_scope("s1relay"):
         relay(10)
         relay(11)
+        for core in range(2):
+            wave_far(2, core).start()
     with jax.named_scope("relay0"):
         relay(0)
     with jax.named_scope("wave0"):
@@ -309,11 +325,13 @@
         finish(11)
         own(16)
         own(17)
+        partner(4)
     with jax.named_scope("p0relay"):
         relay(12)
     with jax.named_scope("s1fin"):
         finish(10, 1)
         own(14)
+        partner(2, (0,))
     with jax.named_scope("relay1"):
         relay(1)
     with jax.named_scope("y0relay"):
@@ -326,7 +344,9 @@
     with jax.named_scope("y1relay"):
         relay(17)
         for core in range(2):
-            wave_far(2, core).start()
+            wave_far(3, core).start()
+        for core in range(2):
+            wave_far(4, core).start()
     with jax.named_scope("relay3"):
         relay(3)
     with jax.named_scope("relay5"):
@@ -335,20 +355,14 @@
         relay(13)
     with jax.named_scope("p0fin"):
         finish(12)
-        partner(0).start()
+        partner(0)
+    with jax.named_scope("y0fin"):
+        finish(16)
+        partner(5)
     with jax.named_scope("p3relay"):
         relay(15)
     with jax.named_scope("relay4"):
         relay(4)
-    with jax.named_scope("y0fin"):
-        finish(16)
-        partner(4).start()
-        finish(17)
-        partner(5).start()
-        for core in range(2):
-            wave_far(3, core).start()
-        for core in range(2):
-            wave_far(4, core).start()
     with jax.named_scope("p2relay"):
         relay(14)
     with jax.named_scope("relay6"):
@@ -358,23 +372,28 @@
         own(7)
     with jax.named_scope("p1fin"):
         finish(13)
-        partner(1).start()
+        partner(1)
+    with jax.named_scope("y1fin"):
+        finish(17)
+        partner(6)
     with jax.named_scope("p3fin"):
         finish(15)
-        partner(3).start()
+        partner(3)
     with jax.named_scope("wave3"):
         wave_in(3).wait_recv()
         own(8)
+    with jax.named_scope("p2fin"):
+        finish(14, 0)
+        partner(2, (1,3))
+        finish(14, 1)
+        partner(2, (2,))
     with jax.named_scope("relay7"):
         relay(7)
-    with jax.named_scope("p2fin"):
-        finish(14)
-        partner(2).start()
+    with jax.named_scope("fw0"):
+        finish_wave(0)
     with jax.named_scope("wave4"):
         wave_in(4).wait_recv()
         own(9)
-    with jax.named_scope("fw0"):
-        finish_wave(0)
     with jax.named_scope("from"):
         bytes_in(rt.at[1 - c], half_sem.at[0])
     with jax.named_scope("b01F"):
@@ -463,7 +482,7 @@
             pltpu.VMEM((NK, 8, 128), F32),
             pltpu.VMEM((8, 128), F32),
             pltpu.VMEM((16, 8, 128), F32),
-            dma((11,)), dma((11,)), dma((NK,)), dma((N_RINGS, 4)), dma((6,)),
+            dma((11,)), dma((11,)), dma((NK,)), dma((46,)), dma((6,)),
         ],
         compiler_params=pltpu.CompilerParams(
             has_side_effects=True, collective_id=0, vmem_limit_bytes=VM

time: 72.5 us -> 70.8 us (0.977)
  Pallas kernels: 70 us -> 68.3 us
    pallas_call x1, Pallas kernels: 70 us -> 68.3 us  [per_device(): pl.pallas_call(kernel, out_shape=(jax.ShapeDtypeStruct((256, 2560), BF16)...]
where the time goes in v5:
time: 70.8 us; the launch traced here: 70.6 us
  Pallas kernels  68.3 us (96%)
  local copies, waits for them, and re-layouts  1.66 us (2%)
    pallas_call x1, Pallas kernels, per_device(): pl.pallas_call(kernel, out_shape=(jax.ShapeDtypeStruct((256, 2560), BF16)...  68.3 us
    unnamed x2, local copies, waits for them, and re-layouts  1.66 us

profile of v5, /device:TPU:1, one launch (start us, length us, event | category | flops | bytes accessed | tf_op | source)
XLA Modules:
  0.0 70.6 jit_solution(13261927748604144777)
XLA Ops:
  0.6 68.3 %rotate.1 = (bf16[256,2560]{1,0:T(8,128)(2,1)S(1)}, f32[20,128]{1,0:T(8,128)S(1)}) custom-call(bf16[256,2560]{1,0:T(8,128)(2,1)} %wave.1, bf16[256,512]{1,0:T(8,128)(2,1)} %ritz.1, f32[1,256]{1,0:T(1,128)} %bitcast.3), custom_call_target="tpu_custom_call" | custom-call | tf_op jit(solution)/shard_map/rotate/pallas_call | solution.py:464
  69.0 1.1 %copy.7 = bf16[256,2560]{1,0:T(8,128)(2,1)} copy(bf16[256,2560]{1,0:T(8,128)(2,1)S(1)} %get-tuple-element.8) | data formatting | bytes 2621440
  70.0 0.6 copy.8

commit v6 on v5

--- a/solution.py
+++ b/solution.py
@@ -18,10 +18,19 @@
 PARTNER_WAVE, FAR_WAVE, SCATTER, SPREAD, RING_X, RING_YZ, CORE, OCC, RESULT, DENSITY, LOCAL = range(11)
 OWN_RESULT, RITZ, OCC_HERE = RING_X, RING_YZ, CORE
 
+def hops(*steps):
+    return sum(min(step, 4 - step) for step in steps)
+
+
 IN_PLANE = sorted(
-    ((dy, dz) for dy in range(4) for dz in range(4) if dy or dz),
-    key=lambda d: -min(d[0], 4 - d[0]) - min(d[1], 4 - d[1]),
+    ((hops(dy, dz), dy, dz) for dy in range(4) for dz in range(4) if dy or dz),
+    key=lambda d: -d[0],
 )
+SHARERS = [
+    (hops(dx, dy), dx, dy, dc)
+    for dx in range(4) for dy in (0, 2) for dc in range(2)
+    if (dx, dy, dc) not in ((0, 0, 0), (0, 2, 0))
+]
 
 
 def at(x, y, z, core):
@@ -246,20 +255,17 @@
                 result_here(k).start()
 
     with jax.named_scope("signal"):
+        peers = [(n, at((x + dx) % 4, (y + dy) % 4, z, (c + dc) % 2)) for n, dx, dy, dc in SHARERS]
+        peers += [(n, at(x, (y + dy) % 4, (z + dz) % 4, c)) for n, dy, dz in IN_PLANE]
+        peers = [peer for _, peer in sorted(peers, key=lambda p: -p[0])]
+        barrier = pltpu.get_barrier_semaphore()
+        for peer in peers:
+            pl.semaphore_signal(barrier, inc=1, device_id=peer, device_id_type=MESH)
         load_ritz = pltpu.make_async_copy(ritz, ritz_here, in_sem.at[RITZ])
         load_occ = pltpu.make_async_copy(occ, occ_here, in_sem.at[OCC_HERE])
         load_ritz.start()
         load_occ.start()
         wave_local().start()
-        peers = []
-        for dy, dz in IN_PLANE:
-            peers.append(at(x, (y + dy) % 4, (z + dz) % 4, c))
-        for d in range(1, 16):
-            if d != 2:
-                peers.append(at((x + d // 4) % 4, (y + 2 * ((d // 2) % 2)) % 4, z, (c + d) % 2))
-        barrier = pltpu.get_barrier_semaphore()
-        for peer in peers:
-            pl.semaphore_signal(barrier, inc=1, device_id=peer, device_id_type=MESH)
 
     with jax.named_scope("transpose"):
         load_ritz.wait()
@@ -273,7 +279,7 @@
         pl.semaphore_wait(barrier, len(peers))
 
     with jax.named_scope("start"):
-        for dy, dz in IN_PLANE:
+        for _, dy, dz in IN_PLANE:
             scatter(dy, dz).start()
         wave_local().wait()
         for p in range(2):
@@ -284,7 +290,6 @@
         bytes_in(wave.at[:, pl.ds(0, 128)], in_sem.at[PARTNER_WAVE])
         own(0)
         bytes_in(wave.at[:, pl.ds(0, 512)], half_sem.at[1])
-        own_first(1)
     with jax.named_scope("scin"):
         bytes_in(w.at[0, pl.ds(0, 192)], in_sem.at[SCATTER])
         for d in (2, 1, 3):
@@ -294,15 +299,15 @@
             wave_far(0, core).start()
         for core in range(2):
             wave_far(1, core).start()
-        own_rest(1)
+        own(1)
         own(2)
         own(3)
         own(4)
     with jax.named_scope("spin"):
         bytes_in(stage.at[pl.ds(0, 3)], in_sem.at[SPREAD])
-        own(10)
         own(11)
         own(12)
+        own(10)
     with jax.named_scope("occ"):
         bytes_in(occ_rows.at[pl.ds(0, 3)], in_sem.at[OCC])
         for s in range(4):
@@ -453,6 +458,19 @@
         bytes_out(dslot.at[pl.ds(0, 15)], out_sem.at[DENSITY])
 
 
+def store(rotated, density, rotated_out, density_out, sem):
+    copies = [pltpu.make_async_copy(density, density_out, sem.at[8])]
+    for i in range(8):
+        rows = pl.ds(i * 32, 32)
+        copies.append(
+            pltpu.make_async_copy(rotated.at[rows], rotated_out.at[rows], sem.at[i])
+        )
+    for copy in copies:
+        copy.start()
+    for copy in copies:
+        copy.wait()
+
+
 def per_device(wave, ritz, occupation):
     wave, ritz, occ = (
         pltpu.with_memory_space_constraint(a, pltpu.HBM)
@@ -489,6 +507,18 @@
         ),
         name="rotate",
     )(wave, ritz, occ)
+    rotated, density = pl.pallas_call(
+        store,
+        out_shape=(
+            jax.ShapeDtypeStruct((256, 2560), BF16),
+            jax.ShapeDtypeStruct((20, 128), F32),
+        ),
+        in_specs=[anywhere, anywhere],
+        out_specs=[pl.BlockSpec(memory_space=pltpu.HBM)] * 2,
+        scratch_shapes=[dma((9,))],
+        compiler_params=pltpu.CompilerParams(vmem_limit_bytes=1024 * 1024),
+        name="store",
+    )(rotated, density)
     return rotated, density.reshape(2560)
 
 

time: 70.8 us -> 69.9 us (0.987)
  local copies, waits for them, and re-layouts: 1.66 us -> 0 us
  Pallas kernels: 68.3 us -> 69.1 us
    unnamed x2 -> x0, local copies, waits for them, and re-layouts: 1.66 us -> none
    pallas_call x0 -> x1, Pallas kernels: none -> 1.13 us  [per_device(): pl.pallas_call(store, out_shape=(jax.ShapeDtypeStruct((256, 2560), BF16),...]
where the time goes in v6:
time: 69.9 us; the launch traced here: 69.7 us
  Pallas kernels  69.1 us (99%)
    pallas_call x1, Pallas kernels, per_device(): pl.pallas_call(kernel, out_shape=(jax.ShapeDtypeStruct((256, 2560), BF16)...  68 us

profile of v6, /device:TPU:1, one launch (start us, length us, event | category | flops | bytes accessed | tf_op | source)
XLA Modules:
  0.0 69.7 jit_solution(17579353486458224706)
XLA Ops:
  0.6 68.0 %rotate.1 = (bf16[256,2560]{1,0:T(8,128)(2,1)S(1)}, f32[20,128]{1,0:T(8,128)S(1)}) custom-call(bf16[256,2560]{1,0:T(8,128)(2,1)} %wave.1, bf16[256,512]{1,0:T(8,128)(2,1)} %ritz.1, f32[1,256]{1,0:T(1,128)} %bitcast.2), custom_call_target="tpu_custom_call" | custom-call | tf_op jit(solution)/shard_map/rotate/pallas_call | solution.py:482
  68.6 1.1 %store.1 = (bf16[256,2560]{1,0:T(8,128)(2,1)}, f32[20,128]{1,0:T(8,128)}) custom-call(bf16[256,2560]{1,0:T(8,128)(2,1)S(1)} %get-tuple-element.6.rotated, f32[20,128]{1,0:T(8,128)S(1)} %get-tuple-element.7.density), custom_call_target="tpu_custom_call" | custom-call | tf_op jit(solution)/shard_map/store/pallas_call | solution.py:510

commit v7 on v6

--- a/solution.py
+++ b/solution.py
@@ -120,9 +120,9 @@
         return block
 
     def sem_of(i, n):
-        if n == 3:
-            return 44 + (i == 14)
-        return i * 2 + n if i < 10 else 20 + (i - 10) * 3 + n
+        if n == 2:
+            return 26 + (i == 14)
+        return i if i < 10 else 10 + (i - 10) * 2 + n
 
     def ring_copy(i, j, v, h):
         block, slot = ring(i), i
@@ -137,11 +137,11 @@
         ref = block((me + v) % 4, h)
         sent = out_sem.at[RING_X if axis == "x" else RING_YZ]
         if j in (0, 3):
-            got = ring_sem.at[sem_of(slot, j // 3)]
+            got = ring_sem.at[sem_of(slot, 0)]
         elif axis == "x":
             got = half_sem.at[2 + max(slot % 5 - 1, 0)]
         else:
-            got = ring_sem.at[sem_of(slot, 3 if slot in (10, 14) and j in (2, 5) else 2)]
+            got = ring_sem.at[sem_of(slot, 2 if slot in (10, 14) and j in (2, 5) else 1)]
         return send(ref, ref, sent, got, device)
 
     def own_first(i):
@@ -157,9 +157,14 @@
         own_rest(i)
 
     def relay(i):
-        ring_copy(i, 0, 3, 0).wait_recv()
+        if i < 10:
+            ref = rt.at[0, 0, 0, pl.ds(0, 2)]
+        elif i in (16, 17):
+            ref = rt.at[c, pl.ds(0, 2), :, 0, :, pl.ds(CA, 2048 - CA)]
+        else:
+            ref = rt.at[c, :, 0, 0, :, pl.ds(CA, 2048 - CA) if i == 11 else pl.ds(0, CA)]
+        bytes_in(ref, ring_sem.at[sem_of(i, 0)])
         ring_copy(i, 2, 3, 0).start()
-        ring_copy(i, 3, 1, 1).wait_recv()
         ring_copy(i, 5, 1, 1).start()
 
     def bytes_in(ref, sem):
@@ -171,31 +176,31 @@
     def finish(i, part=0):
         low, high = pl.ds(0, CA), pl.ds(CA, 2048 - CA)
         if i in (10, 14):
-            bytes_in(rt.at[c, :, 0, 0, :, low], ring_sem.at[sem_of(i, 2 + part)])
+            bytes_in(rt.at[c, :, 0, 0, :, low], ring_sem.at[sem_of(i, 1 + part)])
         elif i == 11:
-            bytes_in(rt.at[c, :, pl.ds(0, 2), 0, :, high], ring_sem.at[sem_of(i, 2)])
+            bytes_in(rt.at[c, :, pl.ds(0, 2), 0, :, high], ring_sem.at[sem_of(i, 1)])
         elif i < 16:
-            bytes_in(rt.at[c, :, pl.ds(0, 2), 0, :, low], ring_sem.at[sem_of(i, 2)])
+            bytes_in(rt.at[c, :, pl.ds(0, 2), 0, :, low], ring_sem.at[sem_of(i, 1)])
         else:
-            bytes_in(rt.at[c, pl.ds(0, 2), :, pl.ds(0, 2), :, high], ring_sem.at[sem_of(i, 2)])
+            bytes_in(rt.at[c, pl.ds(0, 2), :, pl.ds(0, 2), :, high], ring_sem.at[sem_of(i, 1)])
 
     def finish_wave(g):
         bytes_in(rt.at[0, 0, pl.ds(0, 2 if g else 4)], half_sem.at[2 + g])
 
-    def partner(p, vs=()):
-        if p == 2:
-            refs = [rt.at[c, :, (z + v) % 4, (y + 2) % 4, :, pl.ds(0, CA)] for v in vs]
-        elif p < 4:
-            refs = [rt.at[c, :, :, (y + p) % 4, :, pl.ds(0, CA)]]
-        elif p == 4:
-            refs = [rt.at[c, :, :, y, :, pl.ds(CA, 2048 - CA)]]
-        else:
-            refs = [
-                rt.at[c, pl.ds((p - 5) * 2, 2), :, (y + d) % 4, :, pl.ds(CA, 2048 - CA)]
-                for d in range(1, 4)
-            ]
-        for ref in refs:
-            send(ref, ref, out_sem.at[CORE], half_sem.at[0], at(x, y, z, 1 - c)).start()
+    def to_core(ref, sem):
+        send(ref, ref, out_sem.at[CORE], half_sem.at[sem], at(x, y, z, 1 - c)).start()
+
+    def partner(half, d, vs=None):
+        for v in vs or (None,):
+            planes = slice(None) if v is None else (z + v) % 4
+            to_core(
+                rt.at[c, many(2, half), planes, (y + d) % 4, :, pl.ds(0, CA)], 6 if half is near else 0
+            )
+
+    def partner_rest(half, ds):
+        for d in ds:
+            ref = rt.at[c, pl.ds(half * 2, 2), :, (y + d) % 4, :, pl.ds(CA, 2048 - CA)]
+            to_core(ref, ((half + far) % 2) * 6)
 
     def occ_copy(d, src=False):
         yy = y if d == 0 else (y + 2) % 4
@@ -330,13 +335,15 @@
         finish(11)
         own(16)
         own(17)
-        partner(4)
+        partner_rest(0, (0,))
+        partner_rest(1, (0,))
     with jax.named_scope("p0relay"):
         relay(12)
     with jax.named_scope("s1fin"):
         finish(10, 1)
         own(14)
-        partner(2, (0,))
+        partner(far, 2, (0,))
+        partner(near, 2, (0,))
     with jax.named_scope("relay1"):
         relay(1)
     with jax.named_scope("y0relay"):
@@ -360,10 +367,11 @@
         relay(13)
     with jax.named_scope("p0fin"):
         finish(12)
-        partner(0)
+        partner(far, 0)
+        partner(near, 0)
     with jax.named_scope("y0fin"):
         finish(16)
-        partner(5)
+        partner_rest(0, (1,2,3))
     with jax.named_scope("p3relay"):
         relay(15)
     with jax.named_scope("relay4"):
@@ -377,21 +385,24 @@
         own(7)
     with jax.named_scope("p1fin"):
         finish(13)
-        partner(1)
+        partner(far, 1)
+        partner(near, 1)
     with jax.named_scope("y1fin"):
         finish(17)
-        partner(6)
+        partner_rest(1, (1,2,3))
     with jax.named_scope("p3fin"):
         finish(15)
-        partner(3)
+        partner(far, 3)
     with jax.named_scope("wave3"):
         wave_in(3).wait_recv()
         own(8)
     with jax.named_scope("p2fin"):
         finish(14, 0)
-        partner(2, (1,3))
+        partner(far, 2, (1,3))
         finish(14, 1)
-        partner(2, (2,))
+        partner(far, 2, (2,))
+        partner(near, 3)
+        partner(near, 2, (1,2,3))
     with jax.named_scope("relay7"):
         relay(7)
     with jax.named_scope("fw0"):
@@ -400,19 +411,21 @@
         wave_in(4).wait_recv()
         own(9)
     with jax.named_scope("from"):
-        bytes_in(rt.at[1 - c], half_sem.at[0])
+        bytes_in(rt.at[1 - c, pl.ds(0, 2)], half_sem.at[0])
     with jax.named_scope("b01F"):
         blocks((0,1,), far)
     with jax.named_scope("relay8"):
         relay(8)
+    with jax.named_scope("fromN"):
+        bytes_in(rt.at[1 - c, pl.ds(0, 2)], half_sem.at[6])
     with jax.named_scope("b01N"):
         blocks((0,1,), near)
-    with jax.named_scope("relay9"):
-        relay(9)
     with jax.named_scope("fw1"):
         finish_wave(1)
     with jax.named_scope("b2F"):
         blocks((2,), far)
+    with jax.named_scope("relay9"):
+        relay(9)
     with jax.named_scope("b2N"):
         blocks((2,), near)
     with jax.named_scope("fw2"):
@@ -500,7 +513,7 @@
             pltpu.VMEM((NK, 8, 128), F32),
             pltpu.VMEM((8, 128), F32),
             pltpu.VMEM((16, 8, 128), F32),
-            dma((11,)), dma((11,)), dma((NK,)), dma((46,)), dma((6,)),
+            dma((11,)), dma((11,)), dma((NK,)), dma((28,)), dma((7,)),
         ],
         compiler_params=pltpu.CompilerParams(
             has_side_effects=True, collective_id=0, vmem_limit_bytes=VM

time: 69.9 us -> 69.7 us (level)
  no operation moved by 1% of the time
where the time goes in v7:
time: 69.7 us; the launch traced here: 69.6 us
  Pallas kernels  68.9 us (99%)
    pallas_call x1, Pallas kernels, per_device(): pl.pallas_call(kernel, out_shape=(jax.ShapeDtypeStruct((256, 2560), BF16)...  67.8 us

profile of v7, /device:TPU:1, one launch (start us, length us, event | category | flops | bytes accessed | tf_op | source)
XLA Modules:
  0.0 69.6 jit_solution(4035333460668710910)
XLA Ops:
  0.6 67.8 %rotate.1 = (bf16[256,2560]{1,0:T(8,128)(2,1)S(1)}, f32[20,128]{1,0:T(8,128)S(1)}) custom-call(bf16[256,2560]{1,0:T(8,128)(2,1)} %wave.1, bf16[256,512]{1,0:T(8,128)(2,1)} %ritz.1, f32[1,256]{1,0:T(1,128)} %bitcast.2), custom_call_target="tpu_custom_call" | custom-call | tf_op jit(solution)/shard_map/rotate/pallas_call | solution.py:495
  68.4 1.1 %store.1 = (bf16[256,2560]{1,0:T(8,128)(2,1)}, f32[20,128]{1,0:T(8,128)}) custom-call(bf16[256,2560]{1,0:T(8,128)(2,1)S(1)} %get-tuple-element.6.rotated, f32[20,128]{1,0:T(8,128)S(1)} %get-tuple-element.7.density), custom_call_target="tpu_custom_call" | custom-call | tf_op jit(solution)/shard_map/store/pallas_call | solution.py:523

commit v8 on v6

--- a/solution.py
+++ b/solution.py
@@ -120,9 +120,9 @@
         return block
 
     def sem_of(i, n):
-        if n == 3:
-            return 44 + (i == 14)
-        return i * 2 + n if i < 10 else 20 + (i - 10) * 3 + n
+        if n == 2:
+            return 26 + (i == 14)
+        return i if i < 10 else 10 + (i - 10) * 2 + n
 
     def ring_copy(i, j, v, h):
         block, slot = ring(i), i
@@ -137,11 +137,11 @@
         ref = block((me + v) % 4, h)
         sent = out_sem.at[RING_X if axis == "x" else RING_YZ]
         if j in (0, 3):
-            got = ring_sem.at[sem_of(slot, j // 3)]
+            got = ring_sem.at[sem_of(slot, 0)]
         elif axis == "x":
             got = half_sem.at[2 + max(slot % 5 - 1, 0)]
         else:
-            got = ring_sem.at[sem_of(slot, 3 if slot in (10, 14) and j in (2, 5) else 2)]
+            got = ring_sem.at[sem_of(slot, 2 if slot in (10, 14) and j in (2, 5) else 1)]
         return send(ref, ref, sent, got, device)
 
     def own_first(i):
@@ -157,9 +157,14 @@
         own_rest(i)
 
     def relay(i):
-        ring_copy(i, 0, 3, 0).wait_recv()
+        if i < 10:
+            ref = rt.at[0, 0, 0, pl.ds(0, 2)]
+        elif i in (16, 17):
+            ref = rt.at[c, pl.ds(0, 2), :, 0, :, pl.ds(CA, 2048 - CA)]
+        else:
+            ref = rt.at[c, :, 0, 0, :, pl.ds(CA, 2048 - CA) if i == 11 else pl.ds(0, CA)]
+        bytes_in(ref, ring_sem.at[sem_of(i, 0)])
         ring_copy(i, 2, 3, 0).start()
-        ring_copy(i, 3, 1, 1).wait_recv()
         ring_copy(i, 5, 1, 1).start()
 
     def bytes_in(ref, sem):
@@ -171,13 +176,13 @@
     def finish(i, part=0):
         low, high = pl.ds(0, CA), pl.ds(CA, 2048 - CA)
         if i in (10, 14):
-            bytes_in(rt.at[c, :, 0, 0, :, low], ring_sem.at[sem_of(i, 2 + part)])
+            bytes_in(rt.at[c, :, 0, 0, :, low], ring_sem.at[sem_of(i, 1 + part)])
         elif i == 11:
-            bytes_in(rt.at[c, :, pl.ds(0, 2), 0, :, high], ring_sem.at[sem_of(i, 2)])
+            bytes_in(rt.at[c, :, pl.ds(0, 2), 0, :, high], ring_sem.at[sem_of(i, 1)])
         elif i < 16:
-            bytes_in(rt.at[c, :, pl.ds(0, 2), 0, :, low], ring_sem.at[sem_of(i, 2)])
+            bytes_in(rt.at[c, :, pl.ds(0, 2), 0, :, low], ring_sem.at[sem_of(i, 1)])
         else:
-            bytes_in(rt.at[c, pl.ds(0, 2), :, pl.ds(0, 2), :, high], ring_sem.at[sem_of(i, 2)])
+            bytes_in(rt.at[c, pl.ds(0, 2), :, pl.ds(0, 2), :, high], ring_sem.at[sem_of(i, 1)])
 
     def finish_wave(g):
         bytes_in(rt.at[0, 0, pl.ds(0, 2 if g else 4)], half_sem.at[2 + g])
@@ -500,7 +505,7 @@
             pltpu.VMEM((NK, 8, 128), F32),
             pltpu.VMEM((8, 128), F32),
             pltpu.VMEM((16, 8, 128), F32),
-            dma((11,)), dma((11,)), dma((NK,)), dma((46,)), dma((6,)),
+            dma((11,)), dma((11,)), dma((NK,)), dma((28,)), dma((6,)),
         ],
         compiler_params=pltpu.CompilerParams(
             has_side_effects=True, collective_id=0, vmem_limit_bytes=VM

time: 69.9 us -> 69.7 us (level)
  no operation moved by 1% of the time
where the time goes in v8:
time: 69.7 us; the launch traced here: 69.5 us
  Pallas kernels  68.9 us (99%)
    pallas_call x1, Pallas kernels, per_device(): pl.pallas_call(kernel, out_shape=(jax.ShapeDtypeStruct((256, 2560), BF16)...  67.8 us

profile of v8, /device:TPU:1, one launch (start us, length us, event | category | flops | bytes accessed | tf_op | source)
XLA Modules:
  0.0 69.5 jit_solution(17069208593219842476)
XLA Ops:
  0.6 67.8 %rotate.1 = (bf16[256,2560]{1,0:T(8,128)(2,1)S(1)}, f32[20,128]{1,0:T(8,128)S(1)}) custom-call(bf16[256,2560]{1,0:T(8,128)(2,1)} %wave.1, bf16[256,512]{1,0:T(8,128)(2,1)} %ritz.1, f32[1,256]{1,0:T(1,128)} %bitcast.2), custom_call_target="tpu_custom_call" | custom-call | tf_op jit(solution)/shard_map/rotate/pallas_call | solution.py:487
  68.4 1.1 %store.1 = (bf16[256,2560]{1,0:T(8,128)(2,1)}, f32[20,128]{1,0:T(8,128)}) custom-call(bf16[256,2560]{1,0:T(8,128)(2,1)S(1)} %get-tuple-element.6.rotated, f32[20,128]{1,0:T(8,128)S(1)} %get-tuple-element.7.density), custom_call_target="tpu_custom_call" | custom-call | tf_op jit(solution)/shard_map/store/pallas_call | solution.py:515
